TPU v7x, 32 devices: a whole 2x2x4 slice. The times are simulated.
32 devices in a mesh: region: 2 (over x), blk: 16 (over z, y, core).
Axes of the slice: x: 2, y: 2, z: 4, core: 2. Of those that a mesh axis runs over, the one named last changes fastest.
Arguments:
- ensemble: float32 [64, 256, 128], P(('region', 'blk'))
- observed: float32 [64, 256, 128], P(('region', 'blk')), may hold values from -6 to 6
- obs_var: float32 [64, 256], P(('region', 'blk')), may hold values from 0.5 to 2
- ridge: float32 [64], P(('region', 'blk')), may hold values from 0.05 to 0.5
- pred_back: int32 [64, 12], P(('region', 'blk')), may hold values from 0 to 16, as said below
- bounds: float32 [2], replicated, may hold values from 0.2 to 6, as said below
Outputs:
- analysis: float32 [64, 256, 128], P(('region', 'blk'))
Inputs may be any that keep to these rules, and one draw needn't show every extreme that they name: `pred_back`: each row holds distinct distances among 1 to 16, never more than the block's own index, with 0 for an empty slot; the last block fills all 12 slots. bounds[0] < bounds[1].
All inputs are finite; a program needn't handle non-finite values.
Results may differ from a plain program's by a relative error of at most 0.0003.
Values sent between devices are 32-bit elements; how exact they have to be, the bound alone decides.
A program may use at most 192 MiB of HBM per device.

v0:
```python
import jax
import jax.numpy as jnp
from jax import lax
from jax.sharding import PartitionSpec as P

REACH = 16
ITERS = 3


def from_behind(value, axis, steps):
    count = lax.axis_size(axis)
    first, last = (max(0, -steps), min(count, count - steps))
    return lax.ppermute(value, axis, [(source, source + steps) for source in range(first, last)])


def small_solve(gram, target):
    size = gram.shape[0]
    factor = {}
    for block_position in range(size):
        running = gram[block_position, block_position]
        for k in range(block_position):
            running = running - factor[block_position, k] * factor[block_position, k]
        factor[block_position, block_position] = jnp.sqrt(running)
        for i in range(block_position + 1, size):
            running = gram[i, block_position]
            for k in range(block_position):
                running = running - factor[i, k] * factor[block_position, k]
            factor[i, block_position] = running / factor[block_position, block_position]
    forward = []
    for i in range(size):
        running = target[i]
        for k in range(i):
            running = running - factor[i, k] * forward[k]
        forward.append(running / factor[i, i])
    analysis_output = [None] * size
    for i in reversed(range(size)):
        running = forward[i]
        for k in range(i + 1, size):
            running = running - factor[k, i] * analysis_output[k]
        analysis_output[i] = running / factor[i, i]
    return jnp.stack(analysis_output)


def previous_blocks(entry_values, reach_devices):
    pieces = [
        from_behind(entry_values, ("region", "blk"), shift_by)
        for shift_by in range(reach_devices, 0, -1)
    ]
    return jnp.concatenate(pieces, axis=0)


def on_device(ensemble, observed, obs_var, ridge, pred_back, bounds):
    highest = lax.Precision.HIGHEST
    local_blocks, rows, members = ensemble.shape
    slots = pred_back.shape[1]
    reach_devices = -(-REACH // local_blocks)
    before = reach_devices * local_blocks
    anomaly = (ensemble - jnp.mean(ensemble, axis=2, keepdims=True)) / jnp.sqrt(
        jnp.float32(members - 1)
    )
    positions = before + jnp.arange(local_blocks, dtype=jnp.int32)[:, None] - pred_back
    positions = jnp.where(pred_back > 0, positions, before + local_blocks)
    empty_zero_matrix = jnp.zeros((1, rows, members), jnp.float32)

    def extend(entry_values):
        return jnp.concatenate(
            [previous_blocks(entry_values, reach_devices), entry_values, empty_zero_matrix], axis=0
        )

    preds = extend(anomaly)[positions]
    identity = jnp.eye(slots, dtype=jnp.float32)
    gram = jnp.einsum("bjrm,bkrm->jkbr", preds, preds, precision=highest)
    gram = gram + ridge[None, None, :, None] * identity[:, :, None, None]
    target = jnp.einsum("bjrm,brm->jbr", preds, anomaly, precision=highest)
    regression_coefficients = small_solve(gram, target)
    resid = anomaly - jnp.einsum("jbr,bjrm->brm", regression_coefficients, preds, precision=highest)
    inverse_var = 1.0 / (jnp.sum(resid * resid, axis=2) + 1e-05)
    inverse_obs = 1.0 / obs_var
    beta_blocks = jnp.transpose(regression_coefficients, (1, 0, 2))
    lower_bound = bounds[0]
    upper_bound = bounds[1]
    theta = (upper_bound + lower_bound) / 2
    delta = (upper_bound - lower_bound) / 2
    sigma = theta / delta
    rho_now = 1.0 / sigma
    residue = inverse_obs[:, :, None] * (observed - ensemble)
    increment = jnp.zeros_like(ensemble)
    direction = residue / theta
    for step in range(ITERS):
        increment = increment + direction
        extended = extend(direction)
        lower_analysis_output = direction
        for lower_slot in range(slots):
            lower_analysis_output = (
                lower_analysis_output
                - beta_blocks[:, lower_slot, :, None] * extended[positions[:, lower_slot]]
            )
        upper_entry_values = lower_analysis_output * inverse_var[:, :, None]
        window = jnp.zeros((before + local_blocks + 1, rows, members), jnp.float32)
        for slot in range(slots):
            window = window.at[positions[:, slot]].add(
                beta_blocks[:, slot, :, None] * upper_entry_values
            )
        analysis_output = upper_entry_values - window[before : before + local_blocks]
        for shift_by in range(1, reach_devices + 1):
            start = (reach_devices - shift_by) * local_blocks
            analysis_output = analysis_output - from_behind(
                window[start : start + local_blocks], ("region", "blk"), -shift_by
            )
        residue = residue - (analysis_output + inverse_obs[:, :, None] * direction)
        rho_next = 1.0 / (2 * sigma - rho_now)
        direction = rho_next * rho_now * direction + 2 * rho_next / delta * residue
        rho_now = rho_next
    increment = increment + direction
    return ensemble + increment


def solution(mesh):
    return jax.shard_map(
        on_device,
        mesh=mesh,
        in_specs=(
            P(("region", "blk"), None, None),
            P(("region", "blk"), None, None),
            P(("region", "blk"), None),
            P(("region", "blk")),
            P(("region", "blk"), None),
            P(),
        ),
        out_specs=P(("region", "blk"), None, None),
        check_vma=False,
    )
```

profile of v0, /device:TPU:0, one launch (start us, length us, event | category | flops | bytes accessed | tf_op | source)
XLA Modules:
  0.0 834.6 jit_solution(17585946975531921600)
XLA Ops:
  5.6 6.0 collective-permute-start
  11.6 3.6 collective-permute-start.1
  15.2 3.1 collective-permute-start.2
  18.3 3.8 collective-permute-start.3
  22.1 3.5 collective-permute-start.4
  31.4 2.7 collective-permute-start.5
  34.8 2.9 collective-permute-start.6
  38.4 8.4 %collective-permute-start.7 = (f32[2,256,128]{2,1,0:T(8,128)S(1)}, f32[2,256,128]{2,1,0:T(8,128)S(1)}, u32[]{:S(2)}, u32[]{:S(2)}) collective-permute-start(f32[2,256,128]{2,1,0:T(8,128)S(1)} %get-tuple-element.338), channel_id=1, source_target_pairs={{0,1},{1,2},{2,3},{3,4},{4,5},{5,6},{6,7},{7,8},{8,9},{9,10},{10,1... | collective-permute-start | bytes 786440 | tf_op jit(solution)/shard_map/ppermute | solution.py:13
  47.6 15.0 %collective-permute-start.8 = (f32[2,256,128]{2,1,0:T(8,128)S(1)}, f32[2,256,128]{2,1,0:T(8,128)}, u32[]{:S(2)}, u32[]{:S(2)}) collective-permute-start(f32[2,256,128]{2,1,0:T(8,128)S(1)} %get-tuple-element.339), channel_id=1, source_target_pairs={{0,8},{1,9},{2,10},{3,11},{4,12},{5,13},{6,14},{7,15},{8,16},{9,17... | collective-permute-start | bytes 786440 | tf_op jit(solution)/shard_map/ppermute | solution.py:13
  63.3 30.8 %collective-permute-start.9 = (f32[2,256,128]{2,1,0:T(8,128)S(1)}, f32[2,256,128]{2,1,0:T(8,128)}, u32[]{:S(2)}, u32[]{:S(2)}) collective-permute-start(f32[2,256,128]{2,1,0:T(8,128)S(1)} %get-tuple-element.339), channel_id=1, source_target_pairs={{0,7},{1,8},{2,9},{3,10},{4,11},{5,12},{6,13},{7,14},{8,15},{9,16}... | collective-permute-start | bytes 786440 | tf_op jit(solution)/shard_map/ppermute | solution.py:13
  107.2 9.3 %bitcast_add_fusion = f32[12,12,2,256]{0,1,3,2:T(8,128)} fusion(f32[2,12,256,128]{3,2,1,0:T(8,128)S(1)} %bitcast.1005, f32[12,12,2]{0,1,2:T(8,128)S(1)} %broadcast_multiply_fusion.36), kind=kOutput, calls=%fused_computation.79 | convolution fusion | flops 113319936 | bytes 3441792 | tf_op jit(solution)/shard_map/bjrm,bkrm->jkbr/dot_general | solution.py:72
  116.5 64.5 %slice_reduce_fusion.56 = (f32[2,256]{1,0:T(2,128)}, f32[2,256]{1,0:T(2,128)}, f32[2,256]{1,0:T(2,128)}, f32[2,256]{1,0:T(2,128)}, f32[2,256]{1,0:T(2,128)S(1)},...) fusion(f32[12,12,2,256]{0,1,3,2:T(8,128)} %bitcast_add_fusion), kind=kLoop, calls=%fused_computation.173 | loop fusion | bytes 77824 | tf_op jit(solution)/shard_map/slice | solution.py:25
  181.0 50.0 %rsqrt_reduce_fusion = (f32[2,256]{1,0:T(2,128)S(1)}, f32[2,256]{1,0:T(2,128)}, f32[2,256]{1,0:T(2,128)}, f32[2,256]{1,0:T(2,128)}, f32[2,256]{1,0:T(2,128)}, /*...) fusion(f32[12,12,2,256]{0,1,3,2:T(8,128)} %bitcast_add_fusion), kind=kLoop, calls=%fused_computation.200 | loop fusion | bytes 77824 | tf_op jit(solution)/shard_map/sqrt | solution.py:23
  231.0 8.5 %slice_reduce_fusion.75 = (f32[2,256]{1,0:T(2,128)S(1)}, f32[2,256]{1,0:T(2,128)S(1)}, f32[2,256]{1,0:T(2,128)S(1)}) fusion(f32[12,12,2,256]{0,1,3,2:T(8,128)} %bitcast_add_fusion), kind=kLoop, calls=%fused_computation.192 | loop fusion | bytes 12288 | tf_op jit(solution)/shard_map/slice | solution.py:20
  239.6 55.6 %slice_reduce_fusion.42 = (f32[2,256]{1,0:T(2,128)}, f32[2,256]{1,0:T(2,128)}, f32[2,256]{1,0:T(2,128)}, f32[2,256]{1,0:T(2,128)S(1)}, f32[2,256]{1,0:T(2,128)S(...) fusion(f32[12,12,2,256]{0,1,3,2:T(8,128)} %bitcast_add_fusion), kind=kLoop, calls=%fused_computation.159 | loop fusion | bytes 77824 | tf_op jit(solution)/shard_map/slice | solution.py:20
  295.2 51.0 %slice_reduce_fusion.23 = (f32[2,256]{1,0:T(2,128)}, f32[2,256]{1,0:T(2,128)}, f32[2,256]{1,0:T(2,128)}, f32[2,256]{1,0:T(2,128)S(1)}, f32[2,256]{1,0:T(2,128)S(...) fusion(f32[12,12,2,256]{0,1,3,2:T(8,128)} %bitcast_add_fusion), kind=kLoop, calls=%fused_computation.140 | loop fusion | bytes 77824 | tf_op jit(solution)/shard_map/slice | solution.py:20
  346.2 9.5 %fusion.2 = f32[2,256,1,12]{3,2,1,0:T(1,128)} fusion(f32[2,256,128,1]{2,3,1,0:T(1,128)} %bitcast.1008, f32[2,12,256,128]{3,2,1,0:T(8,128)S(1)} %bitcast.1006), kind=kOutput, calls=%fused_computation.75 | convolution fusion | flops 9437184 | bytes 3432448 | tf_op jit(solution)/shard_map/bjrm,brm->jbr/dot_general | solution.py:74
  367.9 6.5 fusion
  433.7 10.0 %collective-permute-done.17 = f32[2,256,128]{2,1,0:T(8,128)} collective-permute-done((f32[2,256,128]{2,1,0:T(8,128)S(1)}, f32[2,256,128]{2,1,0:T(8,128)}, u32[]{:S(2)}, u32[]{:S(2)}) %collective-permute-start.17) | collective-permute-done | bytes 262176 | tf_op jit(solution)/shard_map/ppermute | solution.py:13
  448.1 9.3 %collective-permute-done.19 = f32[2,256,128]{2,1,0:T(8,128)} collective-permute-done((f32[2,256,128]{2,1,0:T(8,128)}, f32[2,256,128]{2,1,0:T(8,128)}, u32[]{:S(2)}, u32[]{:S(2)}) %collective-permute-start.19) | collective-permute-done | bytes 262176 | tf_op jit(solution)/shard_map/ppermute | solution.py:13
  459.4 2.9 collective-permute-done.21
  463.9 32.5 %collective-permute-done.23 = f32[2,256,128]{2,1,0:T(8,128)} collective-permute-done((f32[2,256,128]{2,1,0:T(8,128)}, f32[2,256,128]{2,1,0:T(8,128)}, u32[]{:S(2)}, u32[]{:S(2)}) %collective-permute-start.23) | collective-permute-done | bytes 262176 | tf_op jit(solution)/shard_map/ppermute | solution.py:13
  496.4 2.6 multiply_add_fusion.1
  501.8 5.1 collective-permute-start.26
  506.8 3.1 collective-permute-start.27
  511.3 4.3 collective-permute-start.29
  515.7 4.9 collective-permute-start.30
  520.6 4.5 collective-permute-start.31
  525.2 3.8 collective-permute-done.28
  545.9 3.4 broadcast_multiply_fusion.1
  579.9 18.1 %collective-permute-done.33 = f32[2,256,128]{2,1,0:T(8,128)S(1)} collective-permute-done((f32[2,256,128]{2,1,0:T(8,128)S(1)}, f32[2,256,128]{2,1,0:T(8,128)S(1)}, u32[]{:S(2)}, u32[]{:S(2)}) %collective-permute-start.33) | collective-permute-done | bytes 262176 | tf_op jit(solution)/shard_map/ppermute | solution.py:13
  599.3 3.3 collective-permute-done.34
  604.7 12.6 %collective-permute-done.35 = f32[2,256,128]{2,1,0:T(8,128)} collective-permute-done((f32[2,256,128]{2,1,0:T(8,128)}, f32[2,256,128]{2,1,0:T(8,128)}, u32[]{:S(2)}, u32[]{:S(2)}) %collective-permute-start.35) | collective-permute-done | bytes 262176 | tf_op jit(solution)/shard_map/ppermute | solution.py:13
  619.0 5.5 collective-permute-done.37
  626.5 37.5 %collective-permute-done.39 = f32[2,256,128]{2,1,0:T(8,128)} collective-permute-done((f32[2,256,128]{2,1,0:T(8,128)}, f32[2,256,128]{2,1,0:T(8,128)}, u32[]{:S(2)}, u32[]{:S(2)}) %collective-permute-start.39) | collective-permute-done | bytes 262176 | tf_op jit(solution)/shard_map/ppermute | solution.py:13
  669.2 6.8 collective-permute-start.42
  676.1 3.2 collective-permute-start.43
  680.6 4.3 collective-permute-start.45
  684.9 2.9 collective-permute-start.46
  687.8 5.9 collective-permute-start.47
  693.8 3.3 collective-permute-done.44
  714.0 3.2 broadcast_multiply_fusion
  747.9 17.0 %collective-permute-done.49 = f32[2,256,128]{2,1,0:T(8,128)} collective-permute-done((f32[2,256,128]{2,1,0:T(8,128)S(1)}, f32[2,256,128]{2,1,0:T(8,128)}, u32[]{:S(2)}, u32[]{:S(2)}) %collective-permute-start.49) | collective-permute-done | bytes 262176 | tf_op jit(solution)/shard_map/ppermute | solution.py:13
  766.1 3.0 collective-permute-done.50
  770.5 13.0 %collective-permute-done.51 = f32[2,256,128]{2,1,0:T(8,128)} collective-permute-done((f32[2,256,128]{2,1,0:T(8,128)}, f32[2,256,128]{2,1,0:T(8,128)}, u32[]{:S(2)}, u32[]{:S(2)}) %collective-permute-start.51) | collective-permute-done | bytes 262176 | tf_op jit(solution)/shard_map/ppermute | solution.py:13
  785.2 6.8 collective-permute-done.53
  794.0 37.5 %collective-permute-done.55 = f32[2,256,128]{2,1,0:T(8,128)} collective-permute-done((f32[2,256,128]{2,1,0:T(8,128)}, f32[2,256,128]{2,1,0:T(8,128)}, u32[]{:S(2)}, u32[]{:S(2)}) %collective-permute-start.55) | collective-permute-done | bytes 262176 | tf_op jit(solution)/shard_map/ppermute | solution.py:13
  831.5 2.7 fusion.21
  (317 shorter events, 222.0 us)
Async XLA Ops:
  5.6 25.8 %collective-permute-start = (f32[2,256,128]{2,1,0:T(8,128)S(1)}, f32[2,256,128]{2,1,0:T(8,128)S(1)}, u32[]{:S(2)}, u32[]{:S(2)}) collective-permute-start(f32[2,256,128]{2,1,0:T(8,128)S(1)} %get-tuple-element.338), channel_id=1, source_target_pairs={{0,8},{1,9},{2,10},{3,11},{4,12},{5,13},{6,14},{7,15},{8,16},{9,17... | collective-permute-start | bytes 786440 | tf_op jit(solution)/shard_map/ppermute | solution.py:13
  11.6 23.2 %collective-permute-start.1 = (f32[2,256,128]{2,1,0:T(8,128)S(1)}, f32[2,256,128]{2,1,0:T(8,128)S(1)}, u32[]{:S(2)}, u32[]{:S(2)}) collective-permute-start(f32[2,256,128]{2,1,0:T(8,128)S(1)} %get-tuple-element.338), channel_id=1, source_target_pairs={{0,7},{1,8},{2,9},{3,10},{4,11},{5,12},{6,13},{7,14},{8,15},{9,16}... | collective-permute-start | bytes 786440 | tf_op jit(solution)/shard_map/ppermute | solution.py:13
  15.2 23.2 %collective-permute-start.2 = (f32[2,256,128]{2,1,0:T(8,128)S(1)}, f32[2,256,128]{2,1,0:T(8,128)S(1)}, u32[]{:S(2)}, u32[]{:S(2)}) collective-permute-start(f32[2,256,128]{2,1,0:T(8,128)S(1)} %get-tuple-element.338), channel_id=1, source_target_pairs={{0,6},{1,7},{2,8},{3,9},{4,10},{5,11},{6,12},{7,13},{8,14},{9,15},... | collective-permute-start | bytes 786440 | tf_op jit(solution)/shard_map/ppermute | solution.py:13
  18.3 29.3 %collective-permute-start.3 = (f32[2,256,128]{2,1,0:T(8,128)S(1)}, f32[2,256,128]{2,1,0:T(8,128)S(1)}, u32[]{:S(2)}, u32[]{:S(2)}) collective-permute-start(f32[2,256,128]{2,1,0:T(8,128)S(1)} %get-tuple-element.338), channel_id=1, source_target_pairs={{0,5},{1,6},{2,7},{3,8},{4,9},{5,10},{6,11},{7,12},{8,13},{9,14},{... | collective-permute-start | bytes 786440 | tf_op jit(solution)/shard_map/ppermute | solution.py:13
  22.1 41.1 %collective-permute-start.4 = (f32[2,256,128]{2,1,0:T(8,128)S(1)}, f32[2,256,128]{2,1,0:T(8,128)S(1)}, u32[]{:S(2)}, u32[]{:S(2)}) collective-permute-start(f32[2,256,128]{2,1,0:T(8,128)S(1)} %get-tuple-element.338), channel_id=1, source_target_pairs={{0,4},{1,5},{2,6},{3,7},{4,8},{5,9},{6,10},{7,11},{8,12},{9,13},{1... | collective-permute-start | bytes 786440 | tf_op jit(solution)/shard_map/ppermute | solution.py:13
  31.4 63.4 %collective-permute-start.5 = (f32[2,256,128]{2,1,0:T(8,128)S(1)}, f32[2,256,128]{2,1,0:T(8,128)S(1)}, u32[]{:S(2)}, u32[]{:S(2)}) collective-permute-start(f32[2,256,128]{2,1,0:T(8,128)S(1)} %get-tuple-element.338), channel_id=1, source_target_pairs={{0,3},{1,4},{2,5},{3,6},{4,7},{5,8},{6,9},{7,10},{8,11},{9,12},{10... | collective-permute-start | bytes 786440 | tf_op jit(solution)/shard_map/ppermute | solution.py:13
  34.8 62.7 %collective-permute-start.6 = (f32[2,256,128]{2,1,0:T(8,128)S(1)}, f32[2,256,128]{2,1,0:T(8,128)S(1)}, u32[]{:S(2)}, u32[]{:S(2)}) collective-permute-start(f32[2,256,128]{2,1,0:T(8,128)S(1)} %get-tuple-element.338), channel_id=1, source_target_pairs={{0,2},{1,3},{2,4},{3,5},{4,6},{5,7},{6,8},{7,9},{8,10},{9,11},{10,... | collective-permute-start | bytes 786440 | tf_op jit(solution)/shard_map/ppermute | solution.py:13
  38.4 61.8 %collective-permute-start.7 = (f32[2,256,128]{2,1,0:T(8,128)S(1)}, f32[2,256,128]{2,1,0:T(8,128)S(1)}, u32[]{:S(2)}, u32[]{:S(2)}) collective-permute-start(f32[2,256,128]{2,1,0:T(8,128)S(1)} %get-tuple-element.338), channel_id=1, source_target_pairs={{0,1},{1,2},{2,3},{3,4},{4,5},{5,6},{6,7},{7,8},{8,9},{9,10},{10,1... | collective-permute-start | bytes 786440 | tf_op jit(solution)/shard_map/ppermute | solution.py:13
  47.6 326.9 %collective-permute-start.8 = (f32[2,256,128]{2,1,0:T(8,128)S(1)}, f32[2,256,128]{2,1,0:T(8,128)}, u32[]{:S(2)}, u32[]{:S(2)}) collective-permute-start(f32[2,256,128]{2,1,0:T(8,128)S(1)} %get-tuple-element.339), channel_id=1, source_target_pairs={{0,8},{1,9},{2,10},{3,11},{4,12},{5,13},{6,14},{7,15},{8,16},{9,17... | collective-permute-start | bytes 786440 | tf_op jit(solution)/shard_map/ppermute | solution.py:13
  63.3 314.5 %collective-permute-start.9 = (f32[2,256,128]{2,1,0:T(8,128)S(1)}, f32[2,256,128]{2,1,0:T(8,128)}, u32[]{:S(2)}, u32[]{:S(2)}) collective-permute-start(f32[2,256,128]{2,1,0:T(8,128)S(1)} %get-tuple-element.339), channel_id=1, source_target_pairs={{0,7},{1,8},{2,9},{3,10},{4,11},{5,12},{6,13},{7,14},{8,15},{9,16}... | collective-permute-start | bytes 786440 | tf_op jit(solution)/shard_map/ppermute | solution.py:13
  94.8 285.6 %collective-permute-start.10 = (f32[2,256,128]{2,1,0:T(8,128)S(1)}, f32[2,256,128]{2,1,0:T(8,128)}, u32[]{:S(2)}, u32[]{:S(2)}) collective-permute-start(f32[2,256,128]{2,1,0:T(8,128)S(1)} %get-tuple-element.339), channel_id=1, source_target_pairs={{0,6},{1,7},{2,8},{3,9},{4,10},{5,11},{6,12},{7,13},{8,14},{9,15},... | collective-permute-start | bytes 786440 | tf_op jit(solution)/shard_map/ppermute | solution.py:13
  97.5 286.2 %collective-permute-start.11 = (f32[2,256,128]{2,1,0:T(8,128)S(1)}, f32[2,256,128]{2,1,0:T(8,128)}, u32[]{:S(2)}, u32[]{:S(2)}) collective-permute-start(f32[2,256,128]{2,1,0:T(8,128)S(1)} %get-tuple-element.339), channel_id=1, source_target_pairs={{0,5},{1,6},{2,7},{3,8},{4,9},{5,10},{6,11},{7,12},{8,13},{9,14},{... | collective-permute-start | bytes 786440 | tf_op jit(solution)/shard_map/ppermute | solution.py:13
  100.2 284.4 %collective-permute-start.12 = (f32[2,256,128]{2,1,0:T(8,128)S(1)}, f32[2,256,128]{2,1,0:T(8,128)}, u32[]{:S(2)}, u32[]{:S(2)}) collective-permute-start(f32[2,256,128]{2,1,0:T(8,128)S(1)} %get-tuple-element.339), channel_id=1, source_target_pairs={{0,4},{1,5},{2,6},{3,7},{4,8},{5,9},{6,10},{7,11},{8,12},{9,13},{1... | collective-permute-start | bytes 786440 | tf_op jit(solution)/shard_map/ppermute | solution.py:13
  427.2 16.5 %collective-permute-start.17 = (f32[2,256,128]{2,1,0:T(8,128)S(1)}, f32[2,256,128]{2,1,0:T(8,128)}, u32[]{:S(2)}, u32[]{:S(2)}) collective-permute-start(f32[2,256,128]{2,1,0:T(8,128)S(1)} %get-tuple-element.304), channel_id=1, source_target_pairs={{2,0},{3,1},{4,2},{5,3},{6,4},{7,5},{8,6},{9,7},{10,8},{11,9},{12,... | collective-permute-start | bytes 786440 | tf_op jit(solution)/shard_map/ppermute | solution.py:13
  428.5 16.9 %collective-permute-start.18 = (f32[2,256,128]{2,1,0:T(8,128)S(1)}, f32[2,256,128]{2,1,0:T(8,128)}, u32[]{:S(2)}, u32[]{:S(2)}) collective-permute-start(f32[2,256,128]{2,1,0:T(8,128)S(1)} %get-tuple-element.303), channel_id=1, source_target_pairs={{3,0},{4,1},{5,2},{6,3},{7,4},{8,5},{9,6},{10,7},{11,8},{12,9},{13... | collective-permute-start | bytes 786440 | tf_op jit(solution)/shard_map/ppermute | solution.py:13
  429.8 27.6 %collective-permute-start.19 = (f32[2,256,128]{2,1,0:T(8,128)}, f32[2,256,128]{2,1,0:T(8,128)}, u32[]{:S(2)}, u32[]{:S(2)}) collective-permute-start(f32[2,256,128]{2,1,0:T(8,128)} %get-tuple-element.302), channel_id=1, source_target_pairs={{4,0},{5,1},{6,2},{7,3},{8,4},{9,5},{10,6},{11,7},{12,8},{13,9},{1... | collective-permute-start | bytes 786440 | tf_op jit(solution)/shard_map/ppermute | solution.py:13
  431.1 28.3 %collective-permute-start.20 = (f32[2,256,128]{2,1,0:T(8,128)}, f32[2,256,128]{2,1,0:T(8,128)}, u32[]{:S(2)}, u32[]{:S(2)}) collective-permute-start(f32[2,256,128]{2,1,0:T(8,128)} %get-tuple-element.301), channel_id=1, source_target_pairs={{5,0},{6,1},{7,2},{8,3},{9,4},{10,5},{11,6},{12,7},{13,8},{14,9},{... | collective-permute-start | bytes 786440 | tf_op jit(solution)/shard_map/ppermute | solution.py:13
  432.4 29.9 %collective-permute-start.21 = (f32[2,256,128]{2,1,0:T(8,128)}, f32[2,256,128]{2,1,0:T(8,128)}, u32[]{:S(2)}, u32[]{:S(2)}) collective-permute-start(f32[2,256,128]{2,1,0:T(8,128)} %get-tuple-element.300), channel_id=1, source_target_pairs={{6,0},{7,1},{8,2},{9,3},{10,4},{11,5},{12,6},{13,7},{14,8},{15,9},... | collective-permute-start | bytes 786440 | tf_op jit(solution)/shard_map/ppermute | solution.py:13
  443.7 20.3 %collective-permute-start.22 = (f32[2,256,128]{2,1,0:T(8,128)}, f32[2,256,128]{2,1,0:T(8,128)}, u32[]{:S(2)}, u32[]{:S(2)}) collective-permute-start(f32[2,256,128]{2,1,0:T(8,128)} %get-tuple-element.299), channel_id=1, source_target_pairs={{7,0},{8,1},{9,2},{10,3},{11,4},{12,5},{13,6},{14,7},{15,8},{16,9}... | collective-permute-start | bytes 786440 | tf_op jit(solution)/shard_map/ppermute | solution.py:13
  445.4 51.0 %collective-permute-start.23 = (f32[2,256,128]{2,1,0:T(8,128)}, f32[2,256,128]{2,1,0:T(8,128)}, u32[]{:S(2)}, u32[]{:S(2)}) collective-permute-start(f32[2,256,128]{2,1,0:T(8,128)} %get-tuple-element.298), channel_id=1, source_target_pairs={{8,0},{9,1},{10,2},{11,3},{12,4},{13,5},{14,6},{15,7},{16,8},{17,9... | collective-permute-start | bytes 786440 | tf_op jit(solution)/shard_map/ppermute | solution.py:13
  499.0 12.3 %collective-permute-start.24 = (f32[2,256,128]{2,1,0:T(8,128)S(1)}, f32[2,256,128]{2,1,0:T(8,128)S(1)}, u32[]{:S(2)}, u32[]{:S(2)}) collective-permute-start(f32[2,256,128]{2,1,0:T(8,128)S(1)} %get-tuple-element.102), channel_id=1, source_target_pairs={{0,8},{1,9},{2,10},{3,11},{4,12},{5,13},{6,14},{7,15},{8,16},{9,17... | collective-permute-start | bytes 786440 | tf_op jit(solution)/shard_map/ppermute | solution.py:13
  500.5 15.2 %collective-permute-start.25 = (f32[2,256,128]{2,1,0:T(8,128)S(1)}, f32[2,256,128]{2,1,0:T(8,128)S(1)}, u32[]{:S(2)}, u32[]{:S(2)}) collective-permute-start(f32[2,256,128]{2,1,0:T(8,128)S(1)} %get-tuple-element.102), channel_id=1, source_target_pairs={{0,7},{1,8},{2,9},{3,10},{4,11},{5,12},{6,13},{7,14},{8,15},{9,16}... | collective-permute-start | bytes 786440 | tf_op jit(solution)/shard_map/ppermute | solution.py:13
  501.8 18.8 %collective-permute-start.26 = (f32[2,256,128]{2,1,0:T(8,128)S(1)}, f32[2,256,128]{2,1,0:T(8,128)S(1)}, u32[]{:S(2)}, u32[]{:S(2)}) collective-permute-start(f32[2,256,128]{2,1,0:T(8,128)S(1)} %get-tuple-element.102), channel_id=1, source_target_pairs={{0,6},{1,7},{2,8},{3,9},{4,10},{5,11},{6,12},{7,13},{8,14},{9,15},... | collective-permute-start | bytes 786440 | tf_op jit(solution)/shard_map/ppermute | solution.py:13
  506.8 18.3 %collective-permute-start.27 = (f32[2,256,128]{2,1,0:T(8,128)S(1)}, f32[2,256,128]{2,1,0:T(8,128)S(1)}, u32[]{:S(2)}, u32[]{:S(2)}) collective-permute-start(f32[2,256,128]{2,1,0:T(8,128)S(1)} %get-tuple-element.102), channel_id=1, source_target_pairs={{0,5},{1,6},{2,7},{3,8},{4,9},{5,10},{6,11},{7,12},{8,13},{9,14},{... | collective-permute-start | bytes 786440 | tf_op jit(solution)/shard_map/ppermute | solution.py:13
  510.0 19.0 %collective-permute-start.28 = (f32[2,256,128]{2,1,0:T(8,128)S(1)}, f32[2,256,128]{2,1,0:T(8,128)S(1)}, u32[]{:S(2)}, u32[]{:S(2)}) collective-permute-start(f32[2,256,128]{2,1,0:T(8,128)S(1)} %get-tuple-element.102), channel_id=1, source_target_pairs={{0,4},{1,5},{2,6},{3,7},{4,8},{5,9},{6,10},{7,11},{8,12},{9,13},{1... | collective-permute-start | bytes 786440 | tf_op jit(solution)/shard_map/ppermute | solution.py:13
  511.3 17.7 %collective-permute-start.29 = (f32[2,256,128]{2,1,0:T(8,128)S(1)}, f32[2,256,128]{2,1,0:T(8,128)S(1)}, u32[]{:S(2)}, u32[]{:S(2)}) collective-permute-start(f32[2,256,128]{2,1,0:T(8,128)S(1)} %get-tuple-element.102), channel_id=1, source_target_pairs={{0,3},{1,4},{2,5},{3,6},{4,7},{5,8},{6,9},{7,10},{8,11},{9,12},{10... | collective-permute-start | bytes 786440 | tf_op jit(solution)/shard_map/ppermute | solution.py:13
  515.7 13.4 %collective-permute-start.30 = (f32[2,256,128]{2,1,0:T(8,128)S(1)}, f32[2,256,128]{2,1,0:T(8,128)S(1)}, u32[]{:S(2)}, u32[]{:S(2)}) collective-permute-start(f32[2,256,128]{2,1,0:T(8,128)S(1)} %get-tuple-element.102), channel_id=1, source_target_pairs={{0,2},{1,3},{2,4},{3,5},{4,6},{5,7},{6,8},{7,9},{8,10},{9,11},{10,... | collective-permute-start | bytes 786440 | tf_op jit(solution)/shard_map/ppermute | solution.py:13
  573.4 24.6 %collective-permute-start.33 = (f32[2,256,128]{2,1,0:T(8,128)S(1)}, f32[2,256,128]{2,1,0:T(8,128)S(1)}, u32[]{:S(2)}, u32[]{:S(2)}) collective-permute-start(f32[2,256,128]{2,1,0:T(8,128)S(1)} %get-tuple-element.296), channel_id=1, source_target_pairs={{2,0},{3,1},{4,2},{5,3},{6,4},{7,5},{8,6},{9,7},{10,8},{11,9},{12,... | collective-permute-start | bytes 786440 | tf_op jit(solution)/shard_map/ppermute | solution.py:13
  574.7 27.8 %collective-permute-start.34 = (f32[2,256,128]{2,1,0:T(8,128)S(1)}, f32[2,256,128]{2,1,0:T(8,128)S(1)}, u32[]{:S(2)}, u32[]{:S(2)}) collective-permute-start(f32[2,256,128]{2,1,0:T(8,128)S(1)} %get-tuple-element.295), channel_id=1, source_target_pairs={{3,0},{4,1},{5,2},{6,3},{7,4},{8,5},{9,6},{10,7},{11,8},{12,9},{13... | collective-permute-start | bytes 786440 | tf_op jit(solution)/shard_map/ppermute | solution.py:13
  576.0 41.2 %collective-permute-start.35 = (f32[2,256,128]{2,1,0:T(8,128)}, f32[2,256,128]{2,1,0:T(8,128)}, u32[]{:S(2)}, u32[]{:S(2)}) collective-permute-start(f32[2,256,128]{2,1,0:T(8,128)} %get-tuple-element.294), channel_id=1, source_target_pairs={{4,0},{5,1},{6,2},{7,3},{8,4},{9,5},{10,6},{11,7},{12,8},{13,9},{1... | collective-permute-start | bytes 786440 | tf_op jit(solution)/shard_map/ppermute | solution.py:13
  577.3 41.7 %collective-permute-start.36 = (f32[2,256,128]{2,1,0:T(8,128)}, f32[2,256,128]{2,1,0:T(8,128)}, u32[]{:S(2)}, u32[]{:S(2)}) collective-permute-start(f32[2,256,128]{2,1,0:T(8,128)} %get-tuple-element.293), channel_id=1, source_target_pairs={{5,0},{6,1},{7,2},{8,3},{9,4},{10,5},{11,6},{12,7},{13,8},{14,9},{... | collective-permute-start | bytes 786440 | tf_op jit(solution)/shard_map/ppermute | solution.py:13
  578.6 45.9 %collective-permute-start.37 = (f32[2,256,128]{2,1,0:T(8,128)}, f32[2,256,128]{2,1,0:T(8,128)}, u32[]{:S(2)}, u32[]{:S(2)}) collective-permute-start(f32[2,256,128]{2,1,0:T(8,128)} %get-tuple-element.292), channel_id=1, source_target_pairs={{6,0},{7,1},{8,2},{9,3},{10,4},{11,5},{12,6},{13,7},{14,8},{15,9},... | collective-permute-start | bytes 786440 | tf_op jit(solution)/shard_map/ppermute | solution.py:13
  598.0 28.4 %collective-permute-start.38 = (f32[2,256,128]{2,1,0:T(8,128)}, f32[2,256,128]{2,1,0:T(8,128)}, u32[]{:S(2)}, u32[]{:S(2)}) collective-permute-start(f32[2,256,128]{2,1,0:T(8,128)} %get-tuple-element.291), channel_id=1, source_target_pairs={{7,0},{8,1},{9,2},{10,3},{11,4},{12,5},{13,6},{14,7},{15,8},{16,9}... | collective-permute-start | bytes 786440 | tf_op jit(solution)/shard_map/ppermute | solution.py:13
  603.3 60.6 %collective-permute-start.39 = (f32[2,256,128]{2,1,0:T(8,128)}, f32[2,256,128]{2,1,0:T(8,128)}, u32[]{:S(2)}, u32[]{:S(2)}) collective-permute-start(f32[2,256,128]{2,1,0:T(8,128)} %get-tuple-element.290), channel_id=1, source_target_pairs={{8,0},{9,1},{10,2},{11,3},{12,4},{13,5},{14,6},{15,7},{16,8},{17,9... | collective-permute-start | bytes 786440 | tf_op jit(solution)/shard_map/ppermute | solution.py:13
  666.5 14.1 %collective-permute-start.40 = (f32[2,256,128]{2,1,0:T(8,128)S(1)}, f32[2,256,128]{2,1,0:T(8,128)S(1)}, u32[]{:S(2)}, u32[]{:S(2)}) collective-permute-start(f32[2,256,128]{2,1,0:T(8,128)S(1)} %get-tuple-element.98), channel_id=1, source_target_pairs={{0,8},{1,9},{2,10},{3,11},{4,12},{5,13},{6,14},{7,15},{8,16},{9,17... | collective-permute-start | bytes 786440 | tf_op jit(solution)/shard_map/ppermute | solution.py:13
  667.9 17.0 %collective-permute-start.41 = (f32[2,256,128]{2,1,0:T(8,128)S(1)}, f32[2,256,128]{2,1,0:T(8,128)S(1)}, u32[]{:S(2)}, u32[]{:S(2)}) collective-permute-start(f32[2,256,128]{2,1,0:T(8,128)S(1)} %get-tuple-element.98), channel_id=1, source_target_pairs={{0,7},{1,8},{2,9},{3,10},{4,11},{5,12},{6,13},{7,14},{8,15},{9,16}... | collective-permute-start | bytes 786440 | tf_op jit(solution)/shard_map/ppermute | solution.py:13
  669.2 18.6 %collective-permute-start.42 = (f32[2,256,128]{2,1,0:T(8,128)S(1)}, f32[2,256,128]{2,1,0:T(8,128)S(1)}, u32[]{:S(2)}, u32[]{:S(2)}) collective-permute-start(f32[2,256,128]{2,1,0:T(8,128)S(1)} %get-tuple-element.98), channel_id=1, source_target_pairs={{0,6},{1,7},{2,8},{3,9},{4,10},{5,11},{6,12},{7,13},{8,14},{9,15},... | collective-permute-start | bytes 786440 | tf_op jit(solution)/shard_map/ppermute | solution.py:13
  676.1 17.7 %collective-permute-start.43 = (f32[2,256,128]{2,1,0:T(8,128)S(1)}, f32[2,256,128]{2,1,0:T(8,128)S(1)}, u32[]{:S(2)}, u32[]{:S(2)}) collective-permute-start(f32[2,256,128]{2,1,0:T(8,128)S(1)} %get-tuple-element.98), channel_id=1, source_target_pairs={{0,5},{1,6},{2,7},{3,8},{4,9},{5,10},{6,11},{7,12},{8,13},{9,14},{... | collective-permute-start | bytes 786440 | tf_op jit(solution)/shard_map/ppermute | solution.py:13
  679.2 17.9 %collective-permute-start.44 = (f32[2,256,128]{2,1,0:T(8,128)S(1)}, f32[2,256,128]{2,1,0:T(8,128)S(1)}, u32[]{:S(2)}, u32[]{:S(2)}) collective-permute-start(f32[2,256,128]{2,1,0:T(8,128)S(1)} %get-tuple-element.98), channel_id=1, source_target_pairs={{0,4},{1,5},{2,6},{3,7},{4,8},{5,9},{6,10},{7,11},{8,12},{9,13},{1... | collective-permute-start | bytes 786440 | tf_op jit(solution)/shard_map/ppermute | solution.py:13
  680.6 16.6 %collective-permute-start.45 = (f32[2,256,128]{2,1,0:T(8,128)S(1)}, f32[2,256,128]{2,1,0:T(8,128)S(1)}, u32[]{:S(2)}, u32[]{:S(2)}) collective-permute-start(f32[2,256,128]{2,1,0:T(8,128)S(1)} %get-tuple-element.98), channel_id=1, source_target_pairs={{0,3},{1,4},{2,5},{3,6},{4,7},{5,8},{6,9},{7,10},{8,11},{9,12},{10... | collective-permute-start | bytes 786440 | tf_op jit(solution)/shard_map/ppermute | solution.py:13
  684.9 12.2 %collective-permute-start.46 = (f32[2,256,128]{2,1,0:T(8,128)S(1)}, f32[2,256,128]{2,1,0:T(8,128)S(1)}, u32[]{:S(2)}, u32[]{:S(2)}) collective-permute-start(f32[2,256,128]{2,1,0:T(8,128)S(1)} %get-tuple-element.98), channel_id=1, source_target_pairs={{0,2},{1,3},{2,4},{3,5},{4,6},{5,7},{6,8},{7,9},{8,10},{9,11},{10,... | collective-permute-start | bytes 786440 | tf_op jit(solution)/shard_map/ppermute | solution.py:13
  741.4 23.5 %collective-permute-start.49 = (f32[2,256,128]{2,1,0:T(8,128)S(1)}, f32[2,256,128]{2,1,0:T(8,128)}, u32[]{:S(2)}, u32[]{:S(2)}) collective-permute-start(f32[2,256,128]{2,1,0:T(8,128)S(1)} %get-tuple-element.288), channel_id=1, source_target_pairs={{2,0},{3,1},{4,2},{5,3},{6,4},{7,5},{8,6},{9,7},{10,8},{11,9},{12,... | collective-permute-start | bytes 786440 | tf_op jit(solution)/shard_map/ppermute | solution.py:13
  742.7 26.5 %collective-permute-start.50 = (f32[2,256,128]{2,1,0:T(8,128)S(1)}, f32[2,256,128]{2,1,0:T(8,128)}, u32[]{:S(2)}, u32[]{:S(2)}) collective-permute-start(f32[2,256,128]{2,1,0:T(8,128)S(1)} %get-tuple-element.287), channel_id=1, source_target_pairs={{3,0},{4,1},{5,2},{6,3},{7,4},{8,5},{9,6},{10,7},{11,8},{12,9},{13... | collective-permute-start | bytes 786440 | tf_op jit(solution)/shard_map/ppermute | solution.py:13
  744.0 39.5 %collective-permute-start.51 = (f32[2,256,128]{2,1,0:T(8,128)}, f32[2,256,128]{2,1,0:T(8,128)}, u32[]{:S(2)}, u32[]{:S(2)}) collective-permute-start(f32[2,256,128]{2,1,0:T(8,128)} %get-tuple-element.286), channel_id=1, source_target_pairs={{4,0},{5,1},{6,2},{7,3},{8,4},{9,5},{10,6},{11,7},{12,8},{13,9},{1... | collective-permute-start | bytes 786440 | tf_op jit(solution)/shard_map/ppermute | solution.py:13
  745.3 39.9 %collective-permute-start.52 = (f32[2,256,128]{2,1,0:T(8,128)}, f32[2,256,128]{2,1,0:T(8,128)}, u32[]{:S(2)}, u32[]{:S(2)}) collective-permute-start(f32[2,256,128]{2,1,0:T(8,128)} %get-tuple-element.285), channel_id=1, source_target_pairs={{5,0},{6,1},{7,2},{8,3},{9,4},{10,5},{11,6},{12,7},{13,8},{14,9},{... | collective-permute-start | bytes 786440 | tf_op jit(solution)/shard_map/ppermute | solution.py:13
  746.6 45.4 %collective-permute-start.53 = (f32[2,256,128]{2,1,0:T(8,128)}, f32[2,256,128]{2,1,0:T(8,128)}, u32[]{:S(2)}, u32[]{:S(2)}) collective-permute-start(f32[2,256,128]{2,1,0:T(8,128)} %get-tuple-element.284), channel_id=1, source_target_pairs={{6,0},{7,1},{8,2},{9,3},{10,4},{11,5},{12,6},{13,7},{14,8},{15,9},... | collective-permute-start | bytes 786440 | tf_op jit(solution)/shard_map/ppermute | solution.py:13
  764.9 29.1 %collective-permute-start.54 = (f32[2,256,128]{2,1,0:T(8,128)}, f32[2,256,128]{2,1,0:T(8,128)}, u32[]{:S(2)}, u32[]{:S(2)}) collective-permute-start(f32[2,256,128]{2,1,0:T(8,128)} %get-tuple-element.283), channel_id=1, source_target_pairs={{7,0},{8,1},{9,2},{10,3},{11,4},{12,5},{13,6},{14,7},{15,8},{16,9}... | collective-permute-start | bytes 786440 | tf_op jit(solution)/shard_map/ppermute | solution.py:13
  769.1 62.4 %collective-permute-start.55 = (f32[2,256,128]{2,1,0:T(8,128)}, f32[2,256,128]{2,1,0:T(8,128)}, u32[]{:S(2)}, u32[]{:S(2)}) collective-permute-start(f32[2,256,128]{2,1,0:T(8,128)} %get-tuple-element.282), channel_id=1, source_target_pairs={{8,0},{9,1},{10,2},{11,3},{12,4},{13,5},{14,6},{15,7},{16,8},{17,9... | collective-permute-start | bytes 786440 | tf_op jit(solution)/shard_map/ppermute | solution.py:13
  (44 other events, 1027.2 us)
where the time goes:
time: 843 us; the launch traced here: 835 us
  local copies, waits for them, and re-layouts  302 us (36%)
  waiting for transfers between devices  228 us (27%)
  starting transfers between devices  176 us (21%)
  other arithmetic  97.8 us (12%)
  matrix products  25.3 us (3%)
    ppermute x56, waiting for transfers between devices, from_behind(): lax.ppermute(value, axis, [(source, source + steps) for source in range(f...  228 us
    ppermute x56, starting transfers between devices, from_behind(): lax.ppermute(value, axis, [(source, source + steps) for source in range(f...  176 us
    slice x3, local copies, waits for them, and re-layouts, small_solve(): running = gram[block_position, block_position]  115 us
    slice x1, local copies, waits for them, and re-layouts, small_solve(): running = gram[i, block_position]  64.5 us
    scatter-add x36, other arithmetic, on_device(): window.at[positions[:, slot]]  55.8 us
    sqrt x1, local copies, waits for them, and re-layouts, small_solve(): factor[block_position, block_position] = jnp.sqrt(running)  50 us
    gather x36, local copies, waits for them, and re-layouts, on_device(): extended[positions[:, lower_slot]]  48.7 us
  transfers between devices with their start and end apart: 56, of which 24 were waited for; matrix products, arithmetic and copies ran while one was open for 34% of the time, Pallas kernels for 0%

commit v1 on v0

--- a/solution.py
+++ b/solution.py
@@ -1,6 +1,11 @@
+import functools
+import math
+
 import jax
 import jax.numpy as jnp
 from jax import lax
+from jax.experimental import pallas as pl
+from jax.experimental.pallas import tpu as pltpu
 from jax.sharding import PartitionSpec as P
 
 REACH = 16
@@ -115,9 +120,310 @@
     return ensemble + increment
 
 
+SUB = 8
+LANES = 128
+MESH_ID = pl.DeviceIdType.MESH
+
+
+def place():
+    per = lax.axis_size("blk")
+    me = lax.axis_index("region") * per + lax.axis_index("blk")
+    return per, me
+
+
+def greet(n, per, me):
+    barrier = pltpu.get_barrier_semaphore()
+
+    def signal(i, carry):
+        k = lax.rem(me + i, n)
+        pl.semaphore_signal(
+            barrier, inc=1, device_id=(k // per, lax.rem(k, per)), device_id_type=MESH_ID
+        )
+        return carry
+
+    lax.fori_loop(1, n, signal, 0)
+    pl.semaphore_wait(barrier, n - 1)
+
+
+def copy_to(src, dst, send_sem, recv_sem, k, per):
+    return pltpu.make_async_remote_copy(
+        src_ref=src,
+        dst_ref=dst,
+        send_sem=send_sem,
+        recv_sem=recv_sem,
+        device_id=(k // per, lax.rem(k, per)),
+        device_id_type=MESH_ID,
+    )
+
+
+def to_rows_kernel(n, ens, obs, pack, ens_r, obs_r, pack_r, send_sem, recv_sem):
+    per, me = place()
+    local = ens.shape[0]
+    greet(n, per, me)
+    mine = pl.ds(me * local, local)
+
+    def send_ens(i, carry):
+        k = lax.rem(me + i, n)
+        rows = pl.ds(pl.multiple_of(k * SUB, SUB), SUB)
+        copy_to(ens.at[:, rows, :], ens_r.at[mine], send_sem.at[0], recv_sem.at[0], k, per).start()
+        return carry
+
+    def send_rest(i, carry):
+        k = lax.rem(me + i, n)
+        rows = pl.ds(pl.multiple_of(k * SUB, SUB), SUB)
+        copy_to(pack.at[k], pack_r.at[mine], send_sem.at[1], recv_sem.at[1], k, per).start()
+        copy_to(obs.at[:, rows, :], obs_r.at[mine], send_sem.at[2], recv_sem.at[2], k, per).start()
+        return carry
+
+    lax.fori_loop(1, n, send_ens, 0)
+    lax.fori_loop(1, n, send_rest, 0)
+    own = pl.ds(pl.multiple_of(me * SUB, SUB), SUB)
+    ens_r[mine] = ens[:, own, :]
+    obs_r[mine] = obs[:, own, :]
+    pack_r[mine] = pack[me]
+    other = lax.rem(me + 1, n)
+    sent = pl.ds(0, (n - 1) * SUB)
+    got = pl.ds(0, (n - 1) * local)
+    for which, (a, b) in enumerate(
+        (
+            (ens.at[:, sent, :], ens_r.at[got]),
+            (pack.at[pl.ds(0, n - 1)], pack_r.at[got]),
+            (obs.at[:, sent, :], obs_r.at[got]),
+        )
+    ):
+        copy_to(b, b, send_sem.at[which], recv_sem.at[which], other, per).wait_recv()
+        copy_to(a, a, send_sem.at[which], recv_sem.at[which], other, per).wait_send()
+
+
+def to_blocks_kernel(n, z_r, z, send_sem, recv_sem):
+    per, me = place()
+    local = z.shape[0]
+    greet(n, per, me)
+    own = pl.ds(pl.multiple_of(me * SUB, SUB), SUB)
+
+    def send(i, carry):
+        k = lax.rem(me + i, n)
+        copy_to(
+            z_r.at[pl.ds(k * local, local)], z.at[:, own, :], send_sem, recv_sem, k, per
+        ).start()
+        return carry
+
+    lax.fori_loop(1, n, send, 0)
+    z[:, own, :] = z_r[pl.ds(me * local, local)]
+    other = lax.rem(me + 1, n)
+    a = z_r.at[pl.ds(0, (n - 1) * local)]
+    b = z.at[:, pl.ds(0, (n - 1) * SUB), :]
+    copy_to(b, b, send_sem, recv_sem, other, per).wait_recv()
+    copy_to(a, a, send_sem, recv_sem, other, per).wait_send()
+
+
+def rows_kernel(nb, bounds, ens, obs, pack, z, apad, dpad, upad, res, ivar, iobs, corr, wide):
+    members = ens.shape[2]
+    tile = (SUB, LANES)
+    zero = jnp.zeros(tile, jnp.float32)
+    for i in range(REACH):
+        apad[i] = zero
+        dpad[i] = zero
+        upad[nb + i] = zero
+    x = ens[...]
+    mean = jnp.sum(x, axis=2, keepdims=True) * (1.0 / members)
+    apad[pl.ds(REACH, nb)] = (x - mean) * (1.0 / math.sqrt(members - 1))
+
+    lane = lax.broadcasted_iota(jnp.int32, (nb, LANES), 1)
+    back = lane - lax.broadcasted_iota(jnp.int32, (nb, LANES), 0)
+    for r in range(SUB):
+        lhs = apad[pl.ds(REACH, nb), r, :]
+        rhs = jnp.concatenate([lhs, jnp.zeros((LANES - nb, members), jnp.float32)], axis=0)
+        full = lax.dot_general(
+            lhs,
+            rhs,
+            (((1,), (1,)), ((), ())),
+            precision=lax.Precision.HIGHEST,
+            preferred_element_type=jnp.float32,
+        )
+        for delta in range(REACH + 1):
+            corr[delta, r : r + 1, :] = jnp.sum(
+                jnp.where(back == delta, full, 0.0), axis=0, keepdims=True
+            )
+
+    flat = pack[...].reshape(nb, LANES)
+    turned = jnp.concatenate([flat, jnp.zeros((LANES - nb, LANES), jnp.float32)], axis=0).T
+    obs_rows = turned[0:SUB]
+    on_lane = lax.broadcasted_iota(jnp.int32, tile, 1)
+    chosen = [
+        jnp.broadcast_to(turned[SUB + d : SUB + d + 1], tile) > 0.5 for d in range(REACH)
+    ]
+    at = SUB + REACH
+    ridge = jnp.where(on_lane < nb, jnp.broadcast_to(turned[at : at + 1], tile), 1.0)
+
+    factor = {}
+    inverse = []
+    for j in range(REACH):
+        for i in range(j, REACH):
+            value = pltpu.roll(corr[i - j], j + 1, 1)
+            running = jnp.where(chosen[j], jnp.where(chosen[i], value, 0.0), 0.0)
+            if i == j:
+                running = running + ridge
+            for k in range(j):
+                running = running - factor[i, k] * factor[j, k]
+            if i == j:
+                inverse.append(1.0 / jnp.sqrt(running))
+            else:
+                factor[i, j] = running * inverse[j]
+    forward = []
+    for i in range(REACH):
+        running = jnp.where(chosen[i], corr[i + 1], 0.0)
+        for k in range(i):
+            running = running - factor[i, k] * forward[k]
+        forward.append(running * inverse[i])
+    beta = [None] * REACH
+    for i in reversed(range(REACH)):
+        running = forward[i]
+        for k in range(i + 1, REACH):
+            running = running - factor[k, i] * beta[k]
+        beta[i] = running * inverse[i]
+    for d in range(REACH):
+        for g in range(nb + REACH):
+            wide[g, d] = jnp.broadcast_to(beta[d][:, g : g + 1], tile) if g < nb else zero
+    inverse_obs = 1.0 / jnp.where(on_lane < nb, obs_rows, 1.0)
+    for g in range(nb):
+        iobs[g] = jnp.broadcast_to(inverse_obs[:, g : g + 1], tile)
+
+    def lower(ref, g0):
+        values = [ref[g0 + i] for i in range(REACH + SUB)]
+        outs = []
+        for g in range(SUB):
+            total = values[REACH + g]
+            for d in range(REACH):
+                total = total - wide[g0 + g, d] * values[REACH + g - d - 1]
+            outs.append(total)
+        return outs
+
+    def upper(ref, g0):
+        values = [ref[g0 + i] for i in range(REACH + SUB)]
+        outs = []
+        for g in range(SUB):
+            total = values[g]
+            for d in range(REACH):
+                total = total - wide[g0 + g + d + 1, d] * values[g + d + 1]
+            outs.append(total)
+        return outs
+
+    lo = jnp.full(tile, bounds[0], jnp.float32)
+    hi = jnp.full(tile, bounds[1], jnp.float32)
+    theta = (hi + lo) / 2
+    delta = (hi - lo) / 2
+    sigma = theta / delta
+    rho = 1.0 / sigma
+
+    def start(t, carry):
+        g0 = t * SUB
+        for g, resid in enumerate(lower(apad, g0)):
+            total = jnp.sum(resid * resid, axis=1, keepdims=True) + 1e-05
+            ivar[g0 + g] = jnp.broadcast_to(1.0 / total, tile)
+            rhs = iobs[g0 + g] * (obs[g0 + g] - ens[g0 + g])
+            res[g0 + g] = rhs
+            first = rhs / theta
+            dpad[REACH + g0 + g] = first
+            z[g0 + g] = first
+        return carry
+
+    lax.fori_loop(0, nb // SUB, start, 0)
+    for step in range(ITERS):
+        rho_next = 1.0 / (2 * sigma - rho)
+        keep = rho_next * rho
+        move = 2 * rho_next / delta
+        rho = rho_next
+
+        def down(t, carry):
+            g0 = t * SUB
+            for g, value in enumerate(lower(dpad, g0)):
+                upad[g0 + g] = value * ivar[g0 + g]
+            return carry
+
+        def up(t, carry):
+            g0 = t * SUB
+            for g, value in enumerate(upper(upad, g0)):
+                old = dpad[REACH + g0 + g]
+                left = res[g0 + g] - (value + iobs[g0 + g] * old)
+                fresh = keep * old + move * left
+                res[g0 + g] = left
+                dpad[REACH + g0 + g] = fresh
+                z[g0 + g] = z[g0 + g] + fresh
+            return carry
+
+        lax.fori_loop(0, nb // SUB, down, 0)
+        lax.fori_loop(0, nb // SUB, up, 0)
+
+
+def by_rows(n, ensemble, observed, obs_var, ridge, pred_back, bounds):
+    local, rows, members = ensemble.shape
+    nb = n * local
+    f32 = jnp.float32
+    distance = jnp.arange(1, REACH + 1, dtype=jnp.int32)
+    chosen = jnp.any(pred_back[:, None, :] == distance[None, :, None], axis=2).astype(f32)
+    pack = jnp.concatenate(
+        [
+            jnp.transpose(obs_var.reshape(local, n, SUB), (1, 0, 2)),
+            jnp.broadcast_to(chosen[None], (n, local, REACH)),
+            jnp.broadcast_to(ridge[None, :, None], (n, local, 1)),
+            jnp.zeros((n, local, LANES - SUB - REACH - 1), f32),
+        ],
+        axis=2,
+    ).reshape(n, local, 1, LANES)
+    vmem = pl.BlockSpec(memory_space=pltpu.VMEM)
+    row_shape = jax.ShapeDtypeStruct((nb, SUB, members), f32)
+    ens_r, obs_r, pack_r = pl.pallas_call(
+        functools.partial(to_rows_kernel, n),
+        out_shape=(row_shape, row_shape, jax.ShapeDtypeStruct((nb, 1, LANES), f32)),
+        in_specs=[vmem] * 3,
+        out_specs=(vmem,) * 3,
+        scratch_shapes=[pltpu.SemaphoreType.DMA((3,)), pltpu.SemaphoreType.DMA((3,))],
+        compiler_params=pltpu.CompilerParams(collective_id=0, has_side_effects=True),
+        name="to_rows",
+    )(ensemble, observed, pack)
+    blocks = lambda count: pltpu.VMEM((count, SUB, members), f32)
+    z_r = pl.pallas_call(
+        functools.partial(rows_kernel, nb),
+        out_shape=row_shape,
+        in_specs=[pl.BlockSpec(memory_space=pltpu.SMEM)] + [vmem] * 3,
+        out_specs=vmem,
+        scratch_shapes=[
+            blocks(nb + REACH),
+            blocks(nb + REACH),
+            blocks(nb + REACH),
+            blocks(nb),
+            blocks(nb),
+            blocks(nb),
+            pltpu.VMEM((REACH + 1, SUB, LANES), f32),
+            pltpu.VMEM((nb + REACH, REACH, SUB, LANES), f32),
+        ],
+        compiler_params=pltpu.CompilerParams(vmem_limit_bytes=48 << 20),
+        name="rows",
+    )(bounds, ens_r, obs_r, pack_r)
+    z = pl.pallas_call(
+        functools.partial(to_blocks_kernel, n),
+        out_shape=jax.ShapeDtypeStruct(ensemble.shape, f32),
+        in_specs=[vmem],
+        out_specs=vmem,
+        scratch_shapes=[pltpu.SemaphoreType.DMA, pltpu.SemaphoreType.DMA],
+        compiler_params=pltpu.CompilerParams(collective_id=1, has_side_effects=True),
+        name="to_blocks",
+    )(z_r)
+    return ensemble + z
+
+
+def choose(n, ensemble, *rest):
+    local, rows, members = ensemble.shape
+    fits = rows == n * SUB and members == LANES and n * local + REACH <= LANES
+    if fits and (n * local) % SUB == 0:
+        return by_rows(n, ensemble, *rest)
+    return on_device(ensemble, *rest)
+
+
 def solution(mesh):
     return jax.shard_map(
-        on_device,
+        functools.partial(choose, mesh.size),
         mesh=mesh,
         in_specs=(
             P(("region", "blk"), None, None),

time: 843 us -> 51.3 us (0.06)
  local copies, waits for them, and re-layouts: 302 us -> 6.27 us
  waiting for transfers between devices: 228 us -> 0 us
  starting transfers between devices: 176 us -> 0 us
  other arithmetic: 97.8 us -> 2.63 us
  Pallas kernels: 0 us -> 41.9 us
  matrix products: 25.3 us -> 0 us
    ppermute x56 -> x0, waiting for transfers between devices: 228 us -> none  [from_behind(): lax.ppermute(value, axis, [(source, source + steps) for source in range(f...]
    slice x8 -> x0, local copies, waits for them, and re-layouts: 184 us -> none  [the longest x3 115 us: small_solve(): running = gram[block_position, block_position]]
    ppermute x56 -> x0, starting transfers between devices: 176 us -> none  [from_behind(): lax.ppermute(value, axis, [(source, source + steps) for source in range(f...]
    scatter-add x36 -> x0, other arithmetic: 55.8 us -> none  [on_device(): window.at[positions[:, slot]]]
    gather x37 -> x0, local copies, waits for them, and re-layouts: 51.2 us -> none  [the longest x36 48.7 us: on_device(): extended[positions[:, lower_slot]]]
    sqrt x1 -> x0, local copies, waits for them, and re-layouts: 50 us -> none  [small_solve(): factor[block_position, block_position] = jnp.sqrt(running)]
    pallas_call x0 -> x3, Pallas kernels: none -> 41.9 us  [the longest x1 21.1 us: by_rows(): pl.pallas_call(functools.partial(to_rows_kernel, n), out_shape=(row_shape...]
    dot_general x3 -> x0, matrix products: 25.3 us -> none  [the longest x1 9.53 us: on_device(): target = jnp.einsum('bjrm,brm->jbr', preds, anomaly, precision=highest)]
  transfers between devices with their start and end apart: 56 -> 0, of which waited for: 24 -> 0; matrix products, arithmetic and copies ran while one was open for 34% -> 0% of each run, Pallas kernels for 0% -> 0%
where the time goes in v1:
time: 51.3 us; the launch traced here: 50.9 us
  Pallas kernels  41.9 us (82%)
  local copies, waits for them, and re-layouts  6.27 us (12%)
  other arithmetic  2.63 us (5%)
    pallas_call x1, Pallas kernels, by_rows(): pl.pallas_call(functools.partial(to_rows_kernel, n), out_shape=(row_shape...  21.1 us
    pallas_call x1, Pallas kernels, by_rows(): pl.pallas_call(functools.partial(to_blocks_kernel, n), out_shape=jax.Shap...  13 us
    pallas_call x1, Pallas kernels, by_rows(): pl.pallas_call(functools.partial(rows_kernel, nb), out_shape=row_shape, i...  7.87 us
    unnamed x18, local copies, waits for them, and re-layouts  5.99 us
    add x1, other arithmetic, by_rows(): return ensemble + z  1.68 us

profile of v1, /device:TPU:0, one launch (start us, length us, event | category | flops | bytes accessed | tf_op | source)
XLA Modules:
  0.0 50.9 jit_solution(6333912399890862136)
XLA Ops:
  0.0 0.1 pad.3.clone
  0.1 0.0 copy-start.7
  0.1 0.7 %copy-done.7 = s32[2,12]{1,0:T(2,128)S(1)} copy-done((s32[2,12]{1,0:T(2,128)S(1)}, s32[2,12]{1,0:T(2,128)}, u32[]{:S(2)}) %copy-start.7) | copy-done | bytes 120
  0.8 0.2 compare_reduce_fusion
  1.0 0.0 copy-start.6
  1.0 0.7 %copy-done.6 = f32[2,256]{1,0:T(2,128)S(1)} copy-done((f32[2,256]{1,0:T(2,128)S(1)}, f32[2,256]{1,0:T(2,128)}, u32[]{:S(2)}) %copy-start.6) | copy-done | bytes 2072
  1.6 0.1 reshape.17
  1.8 0.0 copy-start.8
  1.8 0.6 %copy-done.8 = f32[2]{0:T(128)S(1)} copy-done((f32[2]{0:T(128)S(1)}, f32[2]{0:T(128)}, u32[]{:S(2)}) %copy-start.8) | copy-done | bytes 32
  2.4 0.1 broadcast_in_dim.7
  2.5 0.8 %maximum_maximum_fusion = f32[32,2,128]{2,1,0:T(2,128)} fusion(f32[32,2,1]{2,1,0:T(2,128)S(1)} %broadcast_in_dim.7, f32[32,2,16]{2,1,0:T(2,128)S(1)} %broadcast_in_dim.6, f32[32,2,8]{2,1,0:T(2,128)S(1)} %bitcast.5, f32[128]{0:T(128)S(1)} %pad.3.clone), kind=kLoop, calls=%fused_computation | loop fusion | flops 24576 | bytes 39680 | tf_op jit(solution)/shard_map/concatenate | solution.py:365
  3.3 21.1 %to_rows.1 = (f32[64,8,128]{2,1,0:T(8,128)}, f32[64,8,128]{2,1,0:T(8,128)}, f32[64,1,128]{2,1,0:T(1,128)}) custom-call(f32[2,256,128]{2,1,0:T(8,128)} %ens.1, f32[2,256,128]{2,1,0:T(8,128)} %obs.1, f32[32,2,1,128]{3,2,1,0:T(1,128)} %bitcast.4), custom_call_target="tpu_custom_call" | custom-call | tf_op jit(solution)/shard_map/to_rows/pallas_call | solution.py:376
  24.3 0.0 copy-start.4
  24.3 0.6 %copy-done.4 = f32[2]{0:T(128)S(1)} copy-done((f32[2]{0:T(128)S(1)}, f32[2]{0:T(128)}, u32[]{:S(2)}) %copy-start.4) | copy-done | bytes 32
  25.0 0.0 copy-start.1
  25.0 0.9 %copy-done.1 = f32[64,8,128]{2,1,0:T(8,128)S(1)} copy-done((f32[64,8,128]{2,1,0:T(8,128)S(1)}, f32[64,8,128]{2,1,0:T(8,128)}, u32[]{:S(2)}) %copy-start.1) | copy-done | bytes 262168
  25.9 0.0 copy-start.2
  25.9 0.9 %copy-done.2 = f32[64,8,128]{2,1,0:T(8,128)S(1)} copy-done((f32[64,8,128]{2,1,0:T(8,128)S(1)}, f32[64,8,128]{2,1,0:T(8,128)}, u32[]{:S(2)}) %copy-start.2) | copy-done | bytes 262168
  26.9 0.0 copy-start.3
  26.9 0.8 %copy-done.3 = f32[64,1,128]{2,1,0:T(1,128)S(1)} copy-done((f32[64,1,128]{2,1,0:T(1,128)S(1)}, f32[64,1,128]{2,1,0:T(1,128)}, u32[]{:S(2)}) %copy-start.3) | copy-done | bytes 32792
  27.6 7.9 %rows.1.z_r = f32[64,8,128]{2,1,0:T(8,128)S(1)} custom-call(f32[2]{0:T(128)S(1)} %copy-done.4, f32[64,8,128]{2,1,0:T(8,128)S(1)} %copy-done.1, f32[64,8,128]{2,1,0:T(8,128)S(1)} %copy-done.2, f32[64,1,128]{2,1,0:T(1,128)S(1)} %copy-done.3), custom_call_target="tpu_custom_call" | custom-call | tf_op jit(solution)/shard_map/rows/pallas_call | solution.py:386
  35.5 0.0 copy-start
  35.5 0.7 %copy-done = f32[64,8,128]{2,1,0:T(8,128)} copy-done((f32[64,8,128]{2,1,0:T(8,128)}, f32[64,8,128]{2,1,0:T(8,128)S(1)}, u32[]{:S(2)}) %copy-start) | copy-done | bytes 262168
  36.2 0.0 copy-start.5
  36.2 13.0 %to_blocks.1 = f32[2,256,128]{2,1,0:T(8,128)} custom-call(f32[64,8,128]{2,1,0:T(8,128)} %copy-done), custom_call_target="tpu_custom_call" | custom-call | tf_op jit(solution)/shard_map/to_blocks/pallas_call | solution.py:404
  49.2 0.0 copy-done.5
  49.3 1.7 %add.11 = f32[2,256,128]{2,1,0:T(8,128)} add(f32[2,256,128]{2,1,0:T(8,128)S(1)} %copy-done.5, f32[2,256,128]{2,1,0:T(8,128)} %to_blocks.1) | non-fusion elementwise | flops 65536 | bytes 786432 | tf_op jit(solution)/shard_map/add | solution.py:413
  (5 shorter events, 0.1 us)
Async XLA Ops:
  0.1 0.7 %copy-start.7 = (s32[2,12]{1,0:T(2,128)S(1)}, s32[2,12]{1,0:T(2,128)}, u32[]{:S(2)}) copy-start(s32[2,12]{1,0:T(2,128)} %param.10) | copy-start | bytes 292
  1.0 0.7 %copy-start.6 = (f32[2,256]{1,0:T(2,128)S(1)}, f32[2,256]{1,0:T(2,128)}, u32[]{:S(2)}) copy-start(f32[2,256]{1,0:T(2,128)} %param.8) | copy-start | bytes 6148
  1.8 0.7 %copy-start.8 = (f32[2]{0:T(128)S(1)}, f32[2]{0:T(128)}, u32[]{:S(2)}) copy-start(f32[2]{0:T(128)} %param.9) | copy-start | bytes 28
  24.3 0.7 %copy-start.4 = (f32[2]{0:T(128)S(1)}, f32[2]{0:T(128)}, u32[]{:S(2)}) copy-start(f32[2]{0:T(128)} %bounds.1) | copy-start | bytes 28
  25.0 0.9 %copy-start.1 = (f32[64,8,128]{2,1,0:T(8,128)S(1)}, f32[64,8,128]{2,1,0:T(8,128)}, u32[]{:S(2)}) copy-start(f32[64,8,128]{2,1,0:T(8,128)} %get-tuple-element.8.ens) | copy-start | bytes 786436
  25.9 0.9 %copy-start.2 = (f32[64,8,128]{2,1,0:T(8,128)S(1)}, f32[64,8,128]{2,1,0:T(8,128)}, u32[]{:S(2)}) copy-start(f32[64,8,128]{2,1,0:T(8,128)} %get-tuple-element.9.obs) | copy-start | bytes 786436
  26.9 0.8 %copy-start.3 = (f32[64,1,128]{2,1,0:T(1,128)S(1)}, f32[64,1,128]{2,1,0:T(1,128)}, u32[]{:S(2)}) copy-start(f32[64,1,128]{2,1,0:T(1,128)} %get-tuple-element.10.pack) | copy-start | bytes 98308
  35.5 0.7 %copy-start = (f32[64,8,128]{2,1,0:T(8,128)}, f32[64,8,128]{2,1,0:T(8,128)S(1)}, u32[]{:S(2)}) copy-start(f32[64,8,128]{2,1,0:T(8,128)S(1)} %rows.1.z_r) | copy-start | bytes 786436
  36.2 13.0 %copy-start.5 = (f32[2,256,128]{2,1,0:T(8,128)S(1)}, f32[2,256,128]{2,1,0:T(8,128)}, u32[]{:S(2)}) copy-start(f32[2,256,128]{2,1,0:T(8,128)} %ens.1) | copy-start | bytes 786436

commit v2 on v1

--- a/solution.py
+++ b/solution.py
@@ -156,68 +156,99 @@
     )
 
 
-def to_rows_kernel(n, ens, obs, pack, ens_r, obs_r, pack_r, send_sem, recv_sem):
-    per, me = place()
-    local = ens.shape[0]
-    greet(n, per, me)
+def gather_rows(n, per, me, ens, obs, obs_var, ridge, pred_back, pack, ens_r, obs_r, pack_r, sems):
+    send_sem, recv_sem = sems
+    local, rows, members = ens.shape
     mine = pl.ds(me * local, local)
 
     def send_ens(i, carry):
         k = lax.rem(me + i, n)
-        rows = pl.ds(pl.multiple_of(k * SUB, SUB), SUB)
-        copy_to(ens.at[:, rows, :], ens_r.at[mine], send_sem.at[0], recv_sem.at[0], k, per).start()
-        return carry
-
-    def send_rest(i, carry):
+        part = pl.ds(pl.multiple_of(k * SUB, SUB), SUB)
+        copy_to(ens.at[:, part, :], ens_r.at[mine], send_sem.at[0], recv_sem.at[0], k, per).start()
+        return carry
+
+    lax.fori_loop(1, n, send_ens, 0)
+
+    lane = lax.broadcasted_iota(jnp.int32, (1, LANES), 1)
+    groups = LANES // SUB
+    for block in range(local):
+        meta = jnp.where(lane == SUB + REACH, ridge[block], 0.0)
+        for slot in range(pred_back.shape[1]):
+            back = pred_back[block, slot]
+            meta = jnp.where((lane == back + (SUB - 1)) & (lane >= SUB), 1.0, meta)
+        for half in range(rows // LANES):
+            row = obs_var[block : block + 1, half * LANES : (half + 1) * LANES]
+            for k in range(groups):
+                turned = row if k == 0 else pltpu.roll(row, LANES - SUB * k, 1)
+                pack[half * groups + k, block] = jnp.where(lane < SUB, turned, meta)
+
+    def send_pack(i, carry):
         k = lax.rem(me + i, n)
-        rows = pl.ds(pl.multiple_of(k * SUB, SUB), SUB)
         copy_to(pack.at[k], pack_r.at[mine], send_sem.at[1], recv_sem.at[1], k, per).start()
-        copy_to(obs.at[:, rows, :], obs_r.at[mine], send_sem.at[2], recv_sem.at[2], k, per).start()
-        return carry
-
-    lax.fori_loop(1, n, send_ens, 0)
-    lax.fori_loop(1, n, send_rest, 0)
+        return carry
+
+    lax.fori_loop(1, n, send_pack, 0)
+
+    def send_obs(i, carry):
+        k = lax.rem(me + i, n)
+        part = pl.ds(pl.multiple_of(k * SUB, SUB), SUB)
+        copy_to(obs.at[:, part, :], obs_r.at[mine], send_sem.at[2], recv_sem.at[2], k, per).start()
+        return carry
+
+    lax.fori_loop(1, n, send_obs, 0)
     own = pl.ds(pl.multiple_of(me * SUB, SUB), SUB)
     ens_r[mine] = ens[:, own, :]
     obs_r[mine] = obs[:, own, :]
     pack_r[mine] = pack[me]
+
+
+def whole_kernel(
+    n, bounds, ens, obs, obs_var, ridge, pred_back, z,
+    pack, ens_r, obs_r, pack_r, z_r, send_sem, recv_sem,
+    apad, dpad, upad, res, ivar, iobs, corr, wide,
+):
+    per, me = place()
+    local = ens.shape[0]
+    greet(n, per, me)
+    gather_rows(
+        n, per, me, ens, obs, obs_var, ridge, pred_back, pack, ens_r, obs_r, pack_r,
+        (send_sem, recv_sem),
+    )
     other = lax.rem(me + 1, n)
     sent = pl.ds(0, (n - 1) * SUB)
     got = pl.ds(0, (n - 1) * local)
-    for which, (a, b) in enumerate(
-        (
-            (ens.at[:, sent, :], ens_r.at[got]),
-            (pack.at[pl.ds(0, n - 1)], pack_r.at[got]),
-            (obs.at[:, sent, :], obs_r.at[got]),
-        )
-    ):
-        copy_to(b, b, send_sem.at[which], recv_sem.at[which], other, per).wait_recv()
-        copy_to(a, a, send_sem.at[which], recv_sem.at[which], other, per).wait_send()
-
-
-def to_blocks_kernel(n, z_r, z, send_sem, recv_sem):
-    per, me = place()
-    local = z.shape[0]
-    greet(n, per, me)
+    whole = (
+        (ens.at[:, sent, :], ens_r.at[got]),
+        (pack.at[pl.ds(0, n - 1)], pack_r.at[got]),
+        (obs.at[:, sent, :], obs_r.at[got]),
+        (z_r.at[got], z.at[:, sent, :]),
+    )
+
+    def arrived(which):
+        ref = whole[which][1]
+        copy_to(ref, ref, send_sem.at[which], recv_sem.at[which], other, per).wait_recv()
+
+    rows_part(
+        n * local, arrived, bounds, ens_r, obs_r, pack_r, z_r,
+        apad, dpad, upad, res, ivar, iobs, corr, wide,
+    )
     own = pl.ds(pl.multiple_of(me * SUB, SUB), SUB)
 
     def send(i, carry):
         k = lax.rem(me + i, n)
         copy_to(
-            z_r.at[pl.ds(k * local, local)], z.at[:, own, :], send_sem, recv_sem, k, per
+            z_r.at[pl.ds(k * local, local)], z.at[:, own, :], send_sem.at[3], recv_sem.at[3], k, per
         ).start()
         return carry
 
     lax.fori_loop(1, n, send, 0)
     z[:, own, :] = z_r[pl.ds(me * local, local)]
-    other = lax.rem(me + 1, n)
-    a = z_r.at[pl.ds(0, (n - 1) * local)]
-    b = z.at[:, pl.ds(0, (n - 1) * SUB), :]
-    copy_to(b, b, send_sem, recv_sem, other, per).wait_recv()
-    copy_to(a, a, send_sem, recv_sem, other, per).wait_send()
-
-
-def rows_kernel(nb, bounds, ens, obs, pack, z, apad, dpad, upad, res, ivar, iobs, corr, wide):
+    arrived(3)
+    for which, (ref, unused) in enumerate(whole):
+        copy_to(ref, ref, send_sem.at[which], recv_sem.at[which], other, per).wait_send()
+
+
+def rows_part(nb, arrived, bounds, ens, obs, pack, z, apad, dpad, upad, res, ivar, iobs, corr, wide):
     members = ens.shape[2]
     tile = (SUB, LANES)
     zero = jnp.zeros(tile, jnp.float32)
@@ -225,6 +256,7 @@
         apad[i] = zero
         dpad[i] = zero
         upad[nb + i] = zero
+    arrived(0)
     x = ens[...]
     mean = jnp.sum(x, axis=2, keepdims=True) * (1.0 / members)
     apad[pl.ds(REACH, nb)] = (x - mean) * (1.0 / math.sqrt(members - 1))
@@ -246,6 +278,7 @@
                 jnp.where(back == delta, full, 0.0), axis=0, keepdims=True
             )
 
+    arrived(1)
     flat = pack[...].reshape(nb, LANES)
     turned = jnp.concatenate([flat, jnp.zeros((LANES - nb, LANES), jnp.float32)], axis=0).T
     obs_rows = turned[0:SUB]
@@ -309,6 +342,7 @@
             outs.append(total)
         return outs
 
+    arrived(2)
     lo = jnp.full(tile, bounds[0], jnp.float32)
     hi = jnp.full(tile, bounds[1], jnp.float32)
     theta = (hi + lo) / 2
@@ -360,35 +394,22 @@
     local, rows, members = ensemble.shape
     nb = n * local
     f32 = jnp.float32
-    distance = jnp.arange(1, REACH + 1, dtype=jnp.int32)
-    chosen = jnp.any(pred_back[:, None, :] == distance[None, :, None], axis=2).astype(f32)
-    pack = jnp.concatenate(
-        [
-            jnp.transpose(obs_var.reshape(local, n, SUB), (1, 0, 2)),
-            jnp.broadcast_to(chosen[None], (n, local, REACH)),
-            jnp.broadcast_to(ridge[None, :, None], (n, local, 1)),
-            jnp.zeros((n, local, LANES - SUB - REACH - 1), f32),
-        ],
-        axis=2,
-    ).reshape(n, local, 1, LANES)
     vmem = pl.BlockSpec(memory_space=pltpu.VMEM)
-    row_shape = jax.ShapeDtypeStruct((nb, SUB, members), f32)
-    ens_r, obs_r, pack_r = pl.pallas_call(
-        functools.partial(to_rows_kernel, n),
-        out_shape=(row_shape, row_shape, jax.ShapeDtypeStruct((nb, 1, LANES), f32)),
-        in_specs=[vmem] * 3,
-        out_specs=(vmem,) * 3,
-        scratch_shapes=[pltpu.SemaphoreType.DMA((3,)), pltpu.SemaphoreType.DMA((3,))],
-        compiler_params=pltpu.CompilerParams(collective_id=0, has_side_effects=True),
-        name="to_rows",
-    )(ensemble, observed, pack)
+    smem = pl.BlockSpec(memory_space=pltpu.SMEM)
     blocks = lambda count: pltpu.VMEM((count, SUB, members), f32)
-    z_r = pl.pallas_call(
-        functools.partial(rows_kernel, nb),
-        out_shape=row_shape,
-        in_specs=[pl.BlockSpec(memory_space=pltpu.SMEM)] + [vmem] * 3,
+    z = pl.pallas_call(
+        functools.partial(whole_kernel, n),
+        out_shape=jax.ShapeDtypeStruct(ensemble.shape, f32),
+        in_specs=[smem, vmem, vmem, vmem, smem, smem],
         out_specs=vmem,
         scratch_shapes=[
+            pltpu.VMEM((n, local, 1, LANES), f32),
+            blocks(nb),
+            blocks(nb),
+            pltpu.VMEM((nb, 1, LANES), f32),
+            blocks(nb),
+            pltpu.SemaphoreType.DMA((4,)),
+            pltpu.SemaphoreType.DMA((4,)),
             blocks(nb + REACH),
             blocks(nb + REACH),
             blocks(nb + REACH),
@@ -398,18 +419,11 @@
             pltpu.VMEM((REACH + 1, SUB, LANES), f32),
             pltpu.VMEM((nb + REACH, REACH, SUB, LANES), f32),
         ],
-        compiler_params=pltpu.CompilerParams(vmem_limit_bytes=48 << 20),
-        name="rows",
-    )(bounds, ens_r, obs_r, pack_r)
-    z = pl.pallas_call(
-        functools.partial(to_blocks_kernel, n),
-        out_shape=jax.ShapeDtypeStruct(ensemble.shape, f32),
-        in_specs=[vmem],
-        out_specs=vmem,
-        scratch_shapes=[pltpu.SemaphoreType.DMA, pltpu.SemaphoreType.DMA],
-        compiler_params=pltpu.CompilerParams(collective_id=1, has_side_effects=True),
-        name="to_blocks",
-    )(z_r)
+        compiler_params=pltpu.CompilerParams(
+            collective_id=0, has_side_effects=True, vmem_limit_bytes=48 << 20
+        ),
+        name="whole",
+    )(bounds, ensemble, observed, obs_var, ridge, pred_back)
     return ensemble + z
 
 

time: 51.3 us -> 38.7 us (0.75)
  Pallas kernels: 41.9 us -> 33.2 us
  other arithmetic: 2.63 us -> 0.74 us
  local copies, waits for them, and re-layouts: 6.27 us -> 4.57 us
    pallas_call x3 -> x1, Pallas kernels: 41.9 us -> 33.2 us  [by_rows(): pl.pallas_call(functools.partial(whole_kernel, n), out_shape=jax.ShapeDty...]
    unnamed x18 -> x12, local copies, waits for them, and re-layouts: 5.99 us -> 4.57 us
    add x1, other arithmetic: 1.68 us -> 0.74 us  [by_rows(): return ensemble + z]
    concatenate x1 -> x0, other arithmetic: 0.75 us -> none  [by_rows(): jnp.concatenate([jnp.transpose(obs_var.reshape(local, n, SUB), (1, 0, 2))...]
where the time goes in v2:
time: 38.7 us; the launch traced here: 38.5 us
  Pallas kernels  33.2 us (86%)
  local copies, waits for them, and re-layouts  4.57 us (12%)
  other arithmetic  0.74 us (2%)
    pallas_call x1, Pallas kernels, by_rows(): pl.pallas_call(functools.partial(whole_kernel, n), out_shape=jax.ShapeDty...  33.2 us
    unnamed x12, local copies, waits for them, and re-layouts  4.57 us

profile of v2, /device:TPU:0, one launch (start us, length us, event | category | flops | bytes accessed | tf_op | source)
XLA Modules:
  0.0 38.5 jit_solution(16787848716259935129)
XLA Ops:
  0.0 0.0 copy-start
  0.0 0.9 %copy-done = f32[2,256,128]{2,1,0:T(8,128)S(1)} copy-done((f32[2,256,128]{2,1,0:T(8,128)S(1)}, f32[2,256,128]{2,1,0:T(8,128)}, u32[]{:S(2)}) %copy-start) | copy-done | bytes 262168
  1.0 0.0 copy-start.1
  1.0 0.9 %copy-done.1 = f32[2,256,128]{2,1,0:T(8,128)S(1)} copy-done((f32[2,256,128]{2,1,0:T(8,128)S(1)}, f32[2,256,128]{2,1,0:T(8,128)}, u32[]{:S(2)}) %copy-start.1) | copy-done | bytes 262168
  1.9 0.0 copy-start.2
  1.9 0.7 %copy-done.2 = f32[2,256]{1,0:T(2,128)S(1)} copy-done((f32[2,256]{1,0:T(2,128)S(1)}, f32[2,256]{1,0:T(2,128)}, u32[]{:S(2)}) %copy-start.2) | copy-done | bytes 2072
  2.6 0.0 copy-start.3
  2.6 0.7 %copy-done.3 = s32[2,12]{1,0:T(2,128)S(1)} copy-done((s32[2,12]{1,0:T(2,128)S(1)}, s32[2,12]{1,0:T(2,128)}, u32[]{:S(2)}) %copy-start.3) | copy-done | bytes 120
  3.3 0.0 copy-start.4
  3.3 0.7 %copy-done.4 = f32[2]{0:T(128)S(1)} copy-done((f32[2]{0:T(128)S(1)}, f32[2]{0:T(128)}, u32[]{:S(2)}) %copy-start.4) | copy-done | bytes 32
  3.9 0.0 copy-start.5
  3.9 0.7 %copy-done.5 = f32[2]{0:T(128)S(1)} copy-done((f32[2]{0:T(128)S(1)}, f32[2]{0:T(128)}, u32[]{:S(2)}) %copy-start.5) | copy-done | bytes 32
  4.6 33.2 %whole.1 = f32[2,256,128]{2,1,0:T(8,128)S(1)} custom-call(f32[2]{0:T(128)S(1)} %copy-done.4, f32[2,256,128]{2,1,0:T(8,128)S(1)} %copy-done, f32[2,256,128]{2,1,0:T(8,128)S(1)} %copy-done.1, f32[2,256]{1,0:T(2,128)S(1)} %copy-done.2, f32[2]{0:T(128)S(1)} %copy-done.5, s32[2,12]{1,0:T(2,128)S(1)} %copy-done.3), custom_call_target="tpu_custom_call" | custom-call | tf_op jit(solution)/shard_map/whole/pallas_call | solution.py:400
  37.8 0.7 %add.3 = f32[2,256,128]{2,1,0:T(8,128)} add(f32[2,256,128]{2,1,0:T(8,128)S(1)} %copy-done, f32[2,256,128]{2,1,0:T(8,128)S(1)} %whole.1) | non-fusion elementwise | flops 65536 | bytes 786432 | tf_op jit(solution)/shard_map/add | solution.py:427
Async XLA Ops:
  0.0 0.9 %copy-start = (f32[2,256,128]{2,1,0:T(8,128)S(1)}, f32[2,256,128]{2,1,0:T(8,128)}, u32[]{:S(2)}) copy-start(f32[2,256,128]{2,1,0:T(8,128)} %ens.1) | copy-start | bytes 786436
  1.0 0.9 %copy-start.1 = (f32[2,256,128]{2,1,0:T(8,128)S(1)}, f32[2,256,128]{2,1,0:T(8,128)}, u32[]{:S(2)}) copy-start(f32[2,256,128]{2,1,0:T(8,128)} %obs.1) | copy-start | bytes 786436
  1.9 0.7 %copy-start.2 = (f32[2,256]{1,0:T(2,128)S(1)}, f32[2,256]{1,0:T(2,128)}, u32[]{:S(2)}) copy-start(f32[2,256]{1,0:T(2,128)} %obs_var.1) | copy-start | bytes 6148
  2.6 0.7 %copy-start.3 = (s32[2,12]{1,0:T(2,128)S(1)}, s32[2,12]{1,0:T(2,128)}, u32[]{:S(2)}) copy-start(s32[2,12]{1,0:T(2,128)} %pred_back.1) | copy-start | bytes 292
  3.3 0.7 %copy-start.4 = (f32[2]{0:T(128)S(1)}, f32[2]{0:T(128)}, u32[]{:S(2)}) copy-start(f32[2]{0:T(128)} %bounds.1) | copy-start | bytes 28
  3.9 0.7 %copy-start.5 = (f32[2]{0:T(128)S(1)}, f32[2]{0:T(128)}, u32[]{:S(2)}) copy-start(f32[2]{0:T(128)} %ridge.1) | copy-start | bytes 28

commit v3 on v2

--- a/solution.py
+++ b/solution.py
@@ -120,6 +120,7 @@
     return ensemble + increment
 
 
+VMEM_GRANT = 66_700_000
 SUB = 8
 LANES = 128
 MESH_ID = pl.DeviceIdType.MESH
@@ -156,7 +157,7 @@
     )
 
 
-def gather_rows(n, per, me, ens, obs, obs_var, ridge, pred_back, pack, ens_r, obs_r, pack_r, sems):
+def gather_rows(n, per, me, loads, ens, obs, obs_var, ridge, pred_back, pack, ens_r, obs_r, pack_r, sems):
     send_sem, recv_sem = sems
     local, rows, members = ens.shape
     mine = pl.ds(me * local, local)
@@ -167,7 +168,10 @@
         copy_to(ens.at[:, part, :], ens_r.at[mine], send_sem.at[0], recv_sem.at[0], k, per).start()
         return carry
 
+    loads[0].wait()
     lax.fori_loop(1, n, send_ens, 0)
+    for load in loads[1:]:
+        load.wait()
 
     lane = lax.broadcasted_iota(jnp.int32, (1, LANES), 1)
     groups = LANES // SUB
@@ -203,15 +207,30 @@
 
 
 def whole_kernel(
-    n, bounds, ens, obs, obs_var, ridge, pred_back, z,
-    pack, ens_r, obs_r, pack_r, z_r, send_sem, recv_sem,
+    n, bounds_in, ens_in, obs_in, obs_var_in, ridge_in, pred_back_in, z,
+    bounds, ens, obs, obs_var, ridge, pred_back, load_sem, pack, ens_r, obs_r, pack_r, z_r, send_sem, recv_sem,
     apad, dpad, upad, res, ivar, iobs, corr, wide,
 ):
     per, me = place()
     local = ens.shape[0]
+    loads = [
+        pltpu.make_async_copy(src, dst, load_sem.at[i])
+        for i, (src, dst) in enumerate(
+            (
+                (ens_in, ens),
+                (obs_in, obs),
+                (obs_var_in, obs_var),
+                (ridge_in, ridge),
+                (pred_back_in, pred_back),
+                (bounds_in, bounds),
+            )
+        )
+    ]
+    for load in loads:
+        load.start()
     greet(n, per, me)
     gather_rows(
-        n, per, me, ens, obs, obs_var, ridge, pred_back, pack, ens_r, obs_r, pack_r,
+        n, per, me, loads, ens, obs, obs_var, ridge, pred_back, pack, ens_r, obs_r, pack_r,
         (send_sem, recv_sem),
     )
     other = lax.rem(me + 1, n)
@@ -395,14 +414,21 @@
     nb = n * local
     f32 = jnp.float32
     vmem = pl.BlockSpec(memory_space=pltpu.VMEM)
-    smem = pl.BlockSpec(memory_space=pltpu.SMEM)
+    hbm = pl.BlockSpec(memory_space=pltpu.HBM)
     blocks = lambda count: pltpu.VMEM((count, SUB, members), f32)
     z = pl.pallas_call(
         functools.partial(whole_kernel, n),
         out_shape=jax.ShapeDtypeStruct(ensemble.shape, f32),
-        in_specs=[smem, vmem, vmem, vmem, smem, smem],
+        in_specs=[hbm] * 6,
         out_specs=vmem,
         scratch_shapes=[
+            pltpu.SMEM(bounds.shape, f32),
+            pltpu.VMEM(ensemble.shape, f32),
+            pltpu.VMEM(observed.shape, f32),
+            pltpu.VMEM(obs_var.shape, f32),
+            pltpu.SMEM(ridge.shape, f32),
+            pltpu.SMEM(pred_back.shape, jnp.int32),
+            pltpu.SemaphoreType.DMA((6,)),
             pltpu.VMEM((n, local, 1, LANES), f32),
             blocks(nb),
             blocks(nb),
@@ -420,7 +446,7 @@
             pltpu.VMEM((nb + REACH, REACH, SUB, LANES), f32),
         ],
         compiler_params=pltpu.CompilerParams(
-            collective_id=0, has_side_effects=True, vmem_limit_bytes=48 << 20
+            collective_id=0, has_side_effects=True, vmem_limit_bytes=VMEM_GRANT
         ),
         name="whole",
     )(bounds, ensemble, observed, obs_var, ridge, pred_back)

time: 38.7 us -> 35.2 us (0.910)
  local copies, waits for them, and re-layouts: 4.57 us -> 0.01 us
  other arithmetic: 0.74 us -> 1.68 us
    unnamed x12 -> x2, local copies, waits for them, and re-layouts: 4.57 us -> 0.01 us
    add x1, other arithmetic: 0.74 us -> 1.68 us  [by_rows(): return ensemble + z]
where the time goes in v3:
time: 35.2 us; the launch traced here: 35.1 us
  Pallas kernels  33.4 us (95%)
  other arithmetic  1.68 us (5%)
    pallas_call x1, Pallas kernels, by_rows(): pl.pallas_call(functools.partial(whole_kernel, n), out_shape=jax.ShapeDty...  33.4 us
    add x1, other arithmetic, by_rows(): return ensemble + z  1.68 us

profile of v3, /device:TPU:0, one launch (start us, length us, event | category | flops | bytes accessed | tf_op | source)
XLA Modules:
  0.0 35.1 jit_solution(3792961349721396956)
XLA Ops:
  0.0 0.0 copy-start
  0.0 33.4 %whole.1 = f32[2,256,128]{2,1,0:T(8,128)} custom-call(f32[2]{0:T(128)} %bounds_in.1, f32[2,256,128]{2,1,0:T(8,128)} %ens_in.1, f32[2,256,128]{2,1,0:T(8,128)} %obs_in.1, f32[2,256]{1,0:T(2,128)} %obs_var_in.1, f32[2]{0:T(128)} %ridge_in.1, s32[2,12]{1,0:T(2,128)} %pred_back_in.1), custom_call_target="tpu_custom_call" | custom-call | tf_op jit(solution)/shard_map/whole/pallas_call | solution.py:419
  33.4 0.0 copy-done
  33.4 1.7 %add.3 = f32[2,256,128]{2,1,0:T(8,128)} add(f32[2,256,128]{2,1,0:T(8,128)S(1)} %copy-done, f32[2,256,128]{2,1,0:T(8,128)} %whole.1) | non-fusion elementwise | flops 65536 | bytes 786432 | tf_op jit(solution)/shard_map/add | solution.py:453
Async XLA Ops:
  0.0 33.4 %copy-start = (f32[2,256,128]{2,1,0:T(8,128)S(1)}, f32[2,256,128]{2,1,0:T(8,128)}, u32[]{:S(2)}) copy-start(f32[2,256,128]{2,1,0:T(8,128)} %ens_in.1) | copy-start | bytes 786436

commit v4 on v3

--- a/solution.py
+++ b/solution.py
@@ -157,19 +157,23 @@
     )
 
 
+def partners(n, per, me):
+    bits = [(1 << b, lax.rem(me // (1 << b), 2)) for b in range(n.bit_length() - 1)]
+    keep = [weight * bit for weight, bit in bits]
+    flip = [weight * (1 - bit) for weight, bit in bits]
+    for i in sorted(range(1, n), key=lambda i: (-(i % per), -i)):
+        yield sum(flip[b] if (i >> b) & 1 else keep[b] for b in range(len(bits)))
+
+
 def gather_rows(n, per, me, loads, ens, obs, obs_var, ridge, pred_back, pack, ens_r, obs_r, pack_r, sems):
     send_sem, recv_sem = sems
     local, rows, members = ens.shape
     mine = pl.ds(me * local, local)
 
-    def send_ens(i, carry):
-        k = lax.rem(me + i, n)
+    loads[0].wait()
+    for k in partners(n, per, me):
         part = pl.ds(pl.multiple_of(k * SUB, SUB), SUB)
         copy_to(ens.at[:, part, :], ens_r.at[mine], send_sem.at[0], recv_sem.at[0], k, per).start()
-        return carry
-
-    loads[0].wait()
-    lax.fori_loop(1, n, send_ens, 0)
     for load in loads[1:]:
         load.wait()
 
@@ -186,20 +190,12 @@
                 turned = row if k == 0 else pltpu.roll(row, LANES - SUB * k, 1)
                 pack[half * groups + k, block] = jnp.where(lane < SUB, turned, meta)
 
-    def send_pack(i, carry):
-        k = lax.rem(me + i, n)
+    for k in partners(n, per, me):
         copy_to(pack.at[k], pack_r.at[mine], send_sem.at[1], recv_sem.at[1], k, per).start()
-        return carry
-
-    lax.fori_loop(1, n, send_pack, 0)
-
-    def send_obs(i, carry):
-        k = lax.rem(me + i, n)
+
+    for k in partners(n, per, me):
         part = pl.ds(pl.multiple_of(k * SUB, SUB), SUB)
         copy_to(obs.at[:, part, :], obs_r.at[mine], send_sem.at[2], recv_sem.at[2], k, per).start()
-        return carry
-
-    lax.fori_loop(1, n, send_obs, 0)
     own = pl.ds(pl.multiple_of(me * SUB, SUB), SUB)
     ens_r[mine] = ens[:, own, :]
     obs_r[mine] = obs[:, own, :]
@@ -253,14 +249,10 @@
     )
     own = pl.ds(pl.multiple_of(me * SUB, SUB), SUB)
 
-    def send(i, carry):
-        k = lax.rem(me + i, n)
+    for k in partners(n, per, me):
         copy_to(
             z_r.at[pl.ds(k * local, local)], z.at[:, own, :], send_sem.at[3], recv_sem.at[3], k, per
         ).start()
-        return carry
-
-    lax.fori_loop(1, n, send, 0)
     z[:, own, :] = z_r[pl.ds(me * local, local)]
     arrived(3)
     for which, (ref, unused) in enumerate(whole):
@@ -456,7 +448,7 @@
 def choose(n, ensemble, *rest):
     local, rows, members = ensemble.shape
     fits = rows == n * SUB and members == LANES and n * local + REACH <= LANES
-    if fits and (n * local) % SUB == 0:
+    if fits and (n * local) % SUB == 0 and n & (n - 1) == 0:
         return by_rows(n, ensemble, *rest)
     return on_device(ensemble, *rest)
 

time: 35.2 us -> 36.3 us (1.031)
  Pallas kernels: 33.4 us -> 34.5 us
    pallas_call x1, Pallas kernels: 33.4 us -> 34.5 us  [by_rows(): pl.pallas_call(functools.partial(whole_kernel, n), out_shape=jax.ShapeDty...]
where the time goes in v4:
time: 36.3 us; the launch traced here: 36.2 us
  Pallas kernels  34.5 us (95%)
  other arithmetic  1.68 us (5%)
    pallas_call x1, Pallas kernels, by_rows(): pl.pallas_call(functools.partial(whole_kernel, n), out_shape=jax.ShapeDty...  34.5 us
    add x1, other arithmetic, by_rows(): return ensemble + z  1.68 us

profile of v4, /device:TPU:0, one launch (start us, length us, event | category | flops | bytes accessed | tf_op | source)
XLA Modules:
  0.0 36.2 jit_solution(2978589896090185162)
XLA Ops:
  0.0 0.0 copy-start
  0.0 34.5 %whole.1 = f32[2,256,128]{2,1,0:T(8,128)} custom-call(f32[2]{0:T(128)} %bounds_in.1, f32[2,256,128]{2,1,0:T(8,128)} %ens_in.1, f32[2,256,128]{2,1,0:T(8,128)} %obs_in.1, f32[2,256]{1,0:T(2,128)} %obs_var_in.1, f32[2]{0:T(128)} %ridge_in.1, s32[2,12]{1,0:T(2,128)} %pred_back_in.1), custom_call_target="tpu_custom_call" | custom-call | tf_op jit(solution)/shard_map/whole/pallas_call | solution.py:411
  34.5 0.0 copy-done
  34.5 1.7 %add.3 = f32[2,256,128]{2,1,0:T(8,128)} add(f32[2,256,128]{2,1,0:T(8,128)S(1)} %copy-done, f32[2,256,128]{2,1,0:T(8,128)} %whole.1) | non-fusion elementwise | flops 65536 | bytes 786432 | tf_op jit(solution)/shard_map/add | solution.py:445
Async XLA Ops:
  0.0 34.5 %copy-start = (f32[2,256,128]{2,1,0:T(8,128)S(1)}, f32[2,256,128]{2,1,0:T(8,128)}, u32[]{:S(2)}) copy-start(f32[2,256,128]{2,1,0:T(8,128)} %ens_in.1) | copy-start | bytes 786436
